TPU v7x, 32 devices: a whole 2x2x4 slice. The times are simulated.
32 devices in a mesh: groups: 2 (over y), dp: 4 (over z), kv: 4 (over x, core).
Axes of the slice: x: 2, y: 2, z: 4, core: 2. Of those that a mesh axis runs over, the one named last changes fastest.
Arguments:
- queries: bfloat16 [128, 3, 8192], P(('groups', 'dp'), None, 'kv'), parts along dimension 0, may hold values from -12 to 12
- routes: int32 [128, 1], P(('groups', 'dp')), parts along dimension 0, may hold values from 0 to 3; in each aligned block of 16 rows (0 to 15, 16 to 31, ...) at most 8 rows name the same one
- suffix_lengths: int32 [128], P(('groups', 'dp')), parts along dimension 0, may hold values from 128 to 256
- prefix_keys: bfloat16 [8, 2048, 1024], P(('groups', 'dp'), None, 'kv'), parts along dimension 0, may hold values from -8 to 8
- prefix_values: bfloat16 [8, 2048, 1024], P(('groups', 'dp'), None, 'kv'), parts along dimension 0, may hold values from -4.5 to 4.5
- suffix_keys: bfloat16 [128, 256, 1024], P(('groups', 'dp'), None, 'kv'), parts along dimension 0, may hold values from -4.5 to 4.5
- suffix_values: bfloat16 [128, 256, 1024], P(('groups', 'dp'), None, 'kv'), parts along dimension 0, may hold values from -4.5 to 4.5
- new_keys: bfloat16 [128, 3, 1024], P(('groups', 'dp'), None, 'kv'), parts along dimension 0, may hold values from -4.5 to 4.5
- new_values: bfloat16 [128, 3, 1024], P(('groups', 'dp'), None, 'kv'), parts along dimension 0, may hold values from -4.5 to 4.5
- out_weight: bfloat16 [8192, 8192], P('kv', 'dp'), may hold values from -0.0625 to 0.0625
Outputs:
- projected: bfloat16 [128, 3, 8192], P(('groups', 'kv'), None, 'dp'), parts along dimension 0
There are 2 independent parts, one for each index of `groups`. A program takes and returns all parts, laid end to end along the dimension named above; an argument that names none is the same for every part. Nothing has to cross between parts.
Inputs may be any that keep to these rules, and one draw needn't show every extreme that they name: `routes`: among the 16 candidates of one index of dp at most 8 continue the same prompt, and in every draw some prompt receives exactly 8 of them from some index.
All inputs are finite; a program needn't handle non-finite values.
Results may differ from a plain program's by a relative error of at most 0.008.
Values may be sent and summed in bfloat16 or wider, within the bound.
No kernel may reach another device: no remote copies, remote signals or barrier semaphores. Data moves between devices by JAX's collectives and lax.ppermute only.
A program may use at most 128 MiB of HBM per device.

v0:
```python
import functools
import math

import jax
import jax.numpy as jnp
from jax import lax
from jax.experimental import pallas as pl
from jax.experimental.pallas import tpu as pltpu
from jax.sharding import PartitionSpec as P


HD = 128
LANES = 128
F32 = jnp.float32
BF16 = jnp.bfloat16
HIDDEN = -1e30
MIB = 1 << 20
PIECES = 4
HALVES = 2
NT = (((1,), (1,)), ((), ()))


def params(mib):
    return pltpu.CompilerParams(vmem_limit_bytes=mib * MIB)


def cost(flops, nbytes, exps=0):
    return pl.CostEstimate(flops=flops, bytes_accessed=nbytes, transcendentals=exps)


def slots(routes_ref, count, capacity, base):
    names = [routes_ref[c] for c in range(count)]
    found = []
    for c in range(count):
        rank = jnp.int32(0)
        for earlier in range(c):
            rank = rank + (names[earlier] == names[c]).astype(jnp.int32)
        found.append((names[c] ^ base) * capacity + rank)
    return found


def spread(scalars, shape, dim):
    index = lax.broadcasted_iota(jnp.int32, shape, dim)
    out = jnp.full(shape, -1, jnp.int32)
    for c, value in enumerate(scalars):
        out = jnp.where(index == c, value, out)
    return out


def pack_kernel(capacity, relative, routes_ref, q_ref, held_ref, choice_ref, *refs):
    out_refs, (names, sems) = refs[:-2], refs[-2:]
    steps, count, _ = q_ref.shape
    name_copy = pltpu.make_async_copy(routes_ref, names, sems.at[0])
    q_copy = pltpu.make_async_copy(q_ref, held_ref, sems.at[1])
    name_copy.start()
    q_copy.start()
    base = lax.axis_index("dp") if relative else 0
    name_copy.wait()
    found = slots(names, count, capacity, base)
    shape = choice_ref.shape
    choice = spread(found, shape, 0) == lax.broadcasted_iota(jnp.int32, shape, 1)
    choice_ref[...] = choice.astype(BF16)
    shape = shape[::-1]
    placement = (spread(found, shape, 1) == lax.broadcasted_iota(jnp.int32, shape, 0)).astype(BF16)
    q_copy.wait()
    for s in range(steps):
        rows = jnp.dot(placement, held_ref[s], preferred_element_type=F32)
        at = 0
        for ref in out_refs:
            ref[s] = rows[at : at + ref.shape[1]].astype(BF16)
            at += ref.shape[1]


def suffix_kernel(
    group,
    q_ref,
    len_hbm,
    k_hbm,
    v_hbm,
    nk_hbm,
    nv_hbm,
    o_ref,
    l_ref,
    len_ref,
    k_ref,
    v_ref,
    nk_ref,
    nv_ref,
    qs,
    ss,
    ps,
    os,
    ls,
    sems,
):
    pairs = (
        (len_hbm, len_ref),
        (k_hbm, k_ref),
        (nk_hbm, nk_ref),
        (nv_hbm, nv_ref),
        (v_hbm, v_ref),
    )
    copies = [
        pltpu.make_async_copy(source, target, sems.at[i])
        for i, (source, target) in enumerate(pairs)
    ]
    for copy in copies:
        copy.start()
    steps, count, width = q_ref.shape
    heads = width // HD // group
    cached = k_ref.shape[1]
    each = steps * group
    rows = count * each
    scale = 1.0 / math.sqrt(HD)
    to_two = scale * math.log2(math.e)
    for h in range(heads):
        for s in range(steps):
            for g in range(group):
                piece = q_ref[s, :, pl.ds((h * group + g) * HD, HD)].astype(F32)
                qs[pl.ds(h * rows + s * group + g, count, stride=each), :] = piece
    row = lax.broadcasted_iota(jnp.int32, (rows, steps * count), 0).astype(F32)
    column = lax.broadcasted_iota(jnp.int32, (rows, steps * count), 1).astype(F32)
    row_cand = jnp.floor((row + 0.5) * (1.0 / each))
    row_step = jnp.floor((row - row_cand * each + 0.5) * (1.0 / group))
    key_step = jnp.floor((column + 0.5) * (1.0 / count))
    key_cand = column - key_step * count
    visible = (row_cand == key_cand) & (key_step <= row_step)
    position = lax.broadcasted_iota(jnp.int32, (each, cached), 1)
    for copy in copies[:4]:
        copy.wait()
    for h in range(heads):
        for c in range(count):
            qc = qs[pl.ds(h * rows + c * each, each), :].astype(BF16)
            kc = k_ref[c, :, pl.ds(h * HD, HD)]
            score = lax.dot_general(qc, kc, NT, preferred_element_type=F32)
            ss[pl.ds(c * each, each), :] = jnp.where(position < len_ref[c], score, HIDDEN)
        nk = jnp.concatenate([nk_ref[t, :, pl.ds(h * HD, HD)] for t in range(steps)], 0)
        nv = jnp.concatenate([nv_ref[t, :, pl.ds(h * HD, HD)] for t in range(steps)], 0)
        fresh = lax.dot_general(
            qs[pl.ds(h * rows, rows), :].astype(BF16), nk, NT, preferred_element_type=F32
        )
        fresh = jnp.where(visible, fresh, HIDDEN)
        score = ss[...]
        peak = jnp.maximum(
            jnp.max(score, -1, keepdims=True), jnp.max(fresh, -1, keepdims=True)
        )
        weight = jnp.exp2((score - peak) * to_two)
        fresh = jnp.exp2((fresh - peak) * to_two)
        total = jnp.sum(weight, -1, keepdims=True) + jnp.sum(fresh, -1, keepdims=True)
        ps[...] = weight.astype(BF16)
        if h == 0:
            copies[4].wait()
        os[...] = jnp.dot(fresh.astype(BF16), nv, preferred_element_type=F32)
        for c in range(count):
            vc = v_ref[c, :, pl.ds(h * HD, HD)]
            pc = ps[pl.ds(c * each, each), :]
            os[pl.ds(c * each, each), :] += jnp.dot(pc, vc, preferred_element_type=F32)
        os[...] = os[...] / total
        ls[...] = jnp.broadcast_to(peak * scale + jnp.log(total), ls.shape)
        for s in range(steps):
            for g in range(group):
                at = pl.ds(s * group + g, count, stride=each)
                lanes = pl.ds((h * group + g) * HD, HD)
                o_ref[s, :, lanes] = os[at, :]
                l_ref[s, :, lanes] = ls[at, :]


def load_kernel(k_hbm, v_hbm, k_ref, v_ref, sems):
    copies = []
    for source, target in ((k_hbm, k_ref), (v_hbm, v_ref)):
        part = source.shape[0] // PIECES
        for at in range(0, source.shape[0], part):
            pair = source.at[pl.ds(at, part)], target.at[pl.ds(at, part)]
            copies.append(pltpu.make_async_copy(*pair, sems.at[len(copies)]))
    for copy in copies:
        copy.start()
    for copy in copies:
        copy.wait()


def prompt_kernel(group, q_ref, k_ref, v_ref, out_ref):
    steps, size, width = q_ref.shape
    heads = width // HD // group
    all_heads = heads * group
    scale = 1.0 / math.sqrt(HD)
    to_two = scale * math.log2(math.e)
    lane = lax.broadcasted_iota(jnp.int32, (size, LANES), 1)
    place = lax.rem(lane, all_heads)
    logs = [jnp.zeros((size, LANES), F32) for _ in range(steps)]
    for h in range(heads):
        keys = k_ref[:, pl.ds(h * HD, HD)]
        values = v_ref[:, pl.ds(h * HD, HD)]
        q = jnp.concatenate(
            [
                q_ref[s, :, pl.ds((h * group + g) * HD, HD)]
                for s in range(steps)
                for g in range(group)
            ],
            0,
        )
        score = lax.dot_general(q, keys, NT, preferred_element_type=F32)
        peak = jnp.max(score, -1, keepdims=True)
        weight = jnp.exp2((score - peak) * to_two)
        total = jnp.sum(weight, -1, keepdims=True)
        out = jnp.dot(weight.astype(BF16), values, preferred_element_type=F32) / total
        log_total = peak * scale + jnp.log(total)
        for s in range(steps):
            for g in range(group):
                at = (s * group + g) * size
                lanes = pl.ds((h * group + g) * HD, HD)
                out_ref[s, :, lanes] = out[at : at + size].astype(BF16)
                logs[s] = jnp.where(place == h * group + g, log_total[at : at + size], logs[s])
    for s in range(steps):
        high = logs[s].astype(BF16).astype(F32)
        rest = logs[s] - high
        middle = rest.astype(BF16).astype(F32)
        low = rest - middle
        terms = jnp.where(lane < all_heads, high, jnp.where(lane < 2 * all_heads, middle, low))
        out_ref[s, :, pl.ds(width, LANES)] = terms.astype(BF16)


def merge_kernel(blocks, *refs):
    choice_ref, row_refs = refs[0], refs[1 : 1 + blocks]
    own_ref, log_ref, out_ref = refs[1 + blocks :]
    steps, count, width = own_ref.shape
    all_heads = width // HD
    choice = choice_ref[...]
    for s in range(steps):
        rows = jnp.concatenate([ref[s] for ref in row_refs], 0)
        rows = jnp.dot(choice, rows, preferred_element_type=F32)
        terms = rows[:, width:]
        logs = (
            terms[:, :all_heads]
            + terms[:, all_heads : 2 * all_heads]
            + terms[:, 2 * all_heads : 3 * all_heads]
        )
        for h in range(all_heads):
            lanes = slice(h * HD, (h + 1) * HD)
            first = jnp.broadcast_to(logs[:, h : h + 1], (count, HD))
            second = log_ref[s, :, lanes]
            peak = jnp.maximum(first, second)
            first = jnp.exp(first - peak)
            second = jnp.exp(second - peak)
            mixed = (first * rows[:, lanes] + second * own_ref[s, :, lanes]) / (first + second)
            out_ref[s, :, lanes] = mixed.astype(BF16)


def project_kernel(first, own_ref, g1_ref, g2_ref, g3_ref, w_ref, own_out, far_out, beside_out, held):
    steps, count, _ = own_ref.shape
    each = steps * count
    me, mine = lax.axis_index("dp"), lax.axis_index("kv")
    for shift, ref in enumerate((own_ref, g1_ref, g2_ref, g3_ref)):
        place = (me ^ shift) ^ mine
        for s in range(steps):
            held[place, pl.ds(s * count, count), :] = ref[s]
    rows = held[...].reshape(4 * each, held.shape[2])
    outs = (own_out, beside_out.at[0], far_out, beside_out.at[1])
    chunk = 512
    for at in range(0, own_out.shape[2], chunk):
        lanes = pl.ds(at, chunk)
        product = jnp.dot(rows, w_ref[:, pl.ds(first + at, chunk)], preferred_element_type=F32)
        for part, ref in enumerate(outs):
            for s in range(steps):
                row = part * each + s * count
                ref[s, :, lanes] = product[row : row + count].astype(ref.dtype)


def add_kernel(keep_ref, got_ref, send_ref):
    for s in range(keep_ref.shape[0]):
        send_ref[s] = (keep_ref[s] + got_ref[1, s].astype(F32)).astype(BF16)


def swap(values, axis, mask):
    pairs = [(i, i ^ mask) for i in range(lax.axis_size(axis))]
    return lax.ppermute(values, axis, pairs)


def local(
    queries,
    routes,
    suffix_lengths,
    prefix_keys,
    prefix_values,
    suffix_keys,
    suffix_values,
    new_keys,
    new_values,
    out_weight,
):
    owners, parts = lax.axis_size("dp"), lax.axis_size("kv")
    count, steps, width = queries.shape
    kv_width = prefix_keys.shape[2]
    heads = kv_width // HD
    group = width // kv_width
    capacity = max(2, 2 * count // owners)
    direct = owners == parts == 4 and capacity % 8 == 0
    blocks = owners if direct else 1
    size = capacity if direct else owners * capacity
    vmem, hbm = pl.BlockSpec(memory_space=pltpu.VMEM), pl.BlockSpec(memory_space=pltpu.HBM)
    far = lambda values: pltpu.with_memory_space_constraint(values, pltpu.HBM)
    names = routes.reshape(count)

    q, choice, *packed = pl.pallas_call(
        functools.partial(pack_kernel, capacity, direct),
        out_shape=[
            jax.ShapeDtypeStruct((steps, count, width), BF16),
            jax.ShapeDtypeStruct((count, owners * capacity), BF16),
        ]
        + [jax.ShapeDtypeStruct((steps, size, width), BF16)] * blocks,
        in_specs=[hbm, hbm],
        out_specs=[vmem] * (blocks + 2),
        scratch_shapes=[pltpu.SMEM((count,), jnp.int32), pltpu.SemaphoreType.DMA((2,))],
        compiler_params=params(8),
        cost_estimate=cost(2 * steps * owners * capacity * count * width, 1 << 20),
        name="pack",
    )(far(names), far(queries.transpose(1, 0, 2)))

    def all_to_all(values):
        values = values.reshape(steps, owners, capacity, -1)
        moved = lax.all_to_all(values, "dp", split_axis=1, concat_axis=1, tiled=True)
        return moved.reshape(steps, owners * capacity, -1)

    if direct:
        received = [packed[0]] + [swap(packed[i], "dp", i) for i in (1, 2, 3)]
    else:
        received = [all_to_all(packed[0])]

    rows = count * steps * group
    cached = suffix_keys.shape[1]
    new_shape = (steps, count, kv_width)
    keys, values = pl.pallas_call(
        load_kernel,
        out_shape=[jax.ShapeDtypeStruct(prefix_keys.shape[1:], BF16)] * 2,
        in_specs=[hbm] * 2,
        out_specs=[vmem] * 2,
        scratch_shapes=[pltpu.SemaphoreType.DMA((2 * PIECES,))],
        compiler_params=params(4),
        cost_estimate=cost(500_000_000, prefix_keys.size * 4),
        name="load",
    )(far(prefix_keys[0]), far(prefix_values[0]))
    own_rows, own_logs = pl.pallas_call(
        functools.partial(suffix_kernel, group),
        out_shape=[jax.ShapeDtypeStruct((steps, count, width), F32)] * 2,
        in_specs=[vmem] + [hbm] * 5,
        out_specs=[vmem] * 2,
        scratch_shapes=[
            pltpu.SMEM((count,), jnp.int32),
            pltpu.VMEM(suffix_keys.shape, BF16),
            pltpu.VMEM(suffix_keys.shape, BF16),
            pltpu.VMEM(new_shape, BF16),
            pltpu.VMEM(new_shape, BF16),
            pltpu.VMEM((heads * rows, HD), F32),
            pltpu.VMEM((rows, cached), F32),
            pltpu.VMEM((rows, cached), BF16),
            pltpu.VMEM((rows, HD), F32),
            pltpu.VMEM((rows, LANES), F32),
            pltpu.SemaphoreType.DMA((5,)),
        ],
        compiler_params=params(16),
        cost_estimate=cost(3_000_000_000, suffix_keys.size * 4, rows * 512),
        name="suffix",
    )(
        q,
        far(suffix_lengths),
        far(suffix_keys),
        far(suffix_values),
        far(new_keys.transpose(1, 0, 2)),
        far(new_values.transpose(1, 0, 2)),
    )

    prompt = pl.pallas_call(
        functools.partial(prompt_kernel, group),
        out_shape=jax.ShapeDtypeStruct((steps, size, width + LANES), BF16),
        in_specs=[vmem] * 3,
        out_specs=vmem,
        compiler_params=params(12 if direct else 48),
        cost_estimate=cost(4 * size * steps * width * prefix_keys.shape[1], prefix_keys.size * 4),
        name="prompt",
    )
    answers = []
    for asked in received:
        answers.append(prompt(asked, keys, values))
    if direct:
        home = [answers[0]] + [swap(answers[i], "dp", i) for i in (1, 2, 3)]
    else:
        home = [all_to_all(answers[0])]

    attended = pl.pallas_call(
        functools.partial(merge_kernel, blocks),
        out_shape=jax.ShapeDtypeStruct((steps, count, width), BF16),
        in_specs=[vmem] * (blocks + 3),
        out_specs=vmem,
        compiler_params=params(8),
        cost_estimate=cost(2 * steps * owners * capacity * count * width, 2 << 20),
        name="merge",
    )(choice, *home, own_rows, own_logs)

    columns = out_weight.shape[1]
    if not direct:
        block_rows = lax.all_gather(attended, "dp", axis=1, tiled=True)
        product = jnp.dot(
            block_rows.reshape(-1, width), out_weight, preferred_element_type=F32
        ).reshape(steps, -1, columns)
        total = lax.psum_scatter(product, "kv", scatter_dimension=1, tiled=True)
        return total.astype(BF16).transpose(1, 0, 2)

    by_two = swap(attended, "dp", 2)
    by_one = swap(attended, "dp", 1)
    by_three = swap(by_two, "dp", 1)
    half = columns // HALVES
    piece = (steps, count, half)

    def reduced(part):
        own_sum, far_sum, beside = pl.pallas_call(
            functools.partial(project_kernel, part * half),
            out_shape=[
                jax.ShapeDtypeStruct(piece, F32),
                jax.ShapeDtypeStruct(piece, F32),
                jax.ShapeDtypeStruct((2, *piece), BF16),
            ],
            in_specs=[vmem] * 5,
            out_specs=[vmem] * 3,
            scratch_shapes=[pltpu.VMEM((owners, steps * count, width), BF16)],
            compiler_params=params(8),
            cost_estimate=cost(2 * owners * steps * count * width * half, width * half * 2),
        )(attended, by_one, by_two, by_three, out_weight)
        got = swap(beside, "kv", 1)
        sent = pl.pallas_call(
            add_kernel,
            out_shape=jax.ShapeDtypeStruct(piece, BF16),
            in_specs=[vmem] * 2,
            out_specs=vmem,
            compiler_params=params(4),
            cost_estimate=cost(far_sum.size, far_sum.size * 12),
        )(far_sum, got)
        came = swap(sent, "kv", 2)
        return own_sum, got, came

    sums = [reduced(part) for part in range(HALVES)]

    def total_kernel(*refs):
        *in_refs, out_ref = refs
        for part in range(HALVES):
            own_ref, got_ref, came_ref = in_refs[3 * part : 3 * part + 3]
            for s in range(steps):
                total = own_ref[s] + got_ref[0, s].astype(F32) + came_ref[s].astype(F32)
                out_ref[s, :, pl.ds(part * half, half)] = total.astype(BF16)

    total = pl.pallas_call(
        total_kernel,
        out_shape=jax.ShapeDtypeStruct((steps, count, columns), BF16),
        in_specs=[vmem] * (3 * HALVES),
        out_specs=vmem,
        compiler_params=params(8),
        cost_estimate=cost(columns * count * steps, columns * count * steps * 12),
        name="total",
    )(*[value for part in sums for value in part])
    return total.transpose(1, 0, 2)


def solution(mesh):
    placed = (
        P(("groups", "dp"), None, "kv"),
        P(("groups", "dp"), None),
        P(("groups", "dp")),
        P(("groups", "dp"), None, "kv"),
        P(("groups", "dp"), None, "kv"),
        P(("groups", "dp"), None, "kv"),
        P(("groups", "dp"), None, "kv"),
        P(("groups", "dp"), None, "kv"),
        P(("groups", "dp"), None, "kv"),
        P("kv", "dp"),
    )
    return jax.shard_map(
        local,
        mesh=mesh,
        in_specs=placed,
        out_specs=P(("groups", "kv"), None, "dp"),
        check_vma=False,
    )
```

profile of v0, /device:TPU:0, one launch (start us, length us, event | category | flops | bytes accessed | tf_op | source)
XLA Modules:
  0.0 52.6 jit_solution(10585011430524746053)
XLA Ops:
  0.0 1.2 %pack.1 = (bf16[3,16,2048]{2,1,0:T(8,128)(2,1)S(1)}, bf16[16,32]{1,0:T(8,128)(2,1)S(1)}, bf16[3,8,2048]{2,1,0:T(8,128)(2,1)S(1)}, bf16[3,8,2048]{2,1,0:T(8,128)(...) custom-call(s32[16]{0:T(128)} %bitcast.12, bf16[3,16,2048]{2,1,0:T(8,128)(2,1)} %bitcast.11), custom_call_target="tpu_custom_call" | custom-call | flops 6291456 | bytes 1048576 | tf_op jit(solution)/shard_map/pack/pallas_call | solution.py:303
  1.2 5.1 %collective-permute-start.4 = (bf16[3,8,2048]{2,1,0:T(8,128)(2,1)S(1)}, bf16[3,8,2048]{2,1,0:T(8,128)(2,1)S(1)}, u32[]{:S(2)}, u32[]{:S(2)}) collective-permute-start(bf16[3,8,2048]{2,1,0:T(8,128)(2,1)S(1)} %get-tuple-element.27), channel_id=1, source_target_pairs={{0,12},{4,8},{8,4},{12,0},{1,13},{5,9},{9,5},{13,1},{2,14},{6,10},... | collective-permute-start | bytes 294920 | tf_op jit(solution)/shard_map/ppermute | solution.py:275
  6.3 0.0 collective-permute-start.2
  6.3 0.6 %collective-permute-start = (bf16[3,8,2048]{2,1,0:T(8,128)(2,1)S(1)}, bf16[3,8,2048]{2,1,0:T(8,128)(2,1)S(1)}, u32[]{:S(2)}, u32[]{:S(2)}) collective-permute-start(bf16[3,8,2048]{2,1,0:T(8,128)(2,1)S(1)} %get-tuple-element.25), channel_id=1, source_target_pairs={{0,4},{4,0},{8,12},{12,8},{1,5},{5,1},{9,13},{13,9},{2,6},{6,2},{1... | collective-permute-start | bytes 294920 | tf_op jit(solution)/shard_map/ppermute | solution.py:275
  7.0 1.6 %load.1 = (bf16[2048,256]{1,0:T(8,128)(2,1)S(1)}, bf16[2048,256]{1,0:T(8,128)(2,1)S(1)}) custom-call(bf16[2048,256]{1,0:T(8,128)(2,1)} %bitcast.9, bf16[2048,256]{1,0:T(8,128)(2,1)} %bitcast.10), custom_call_target="tpu_custom_call" | custom-call | flops 500000000 | bytes 2097152 | tf_op jit(solution)/shard_map/load/pallas_call | solution.py:331
  8.5 1.5 %collective-permute-done.4.q_ref = bf16[3,8,2048]{2,1,0:T(8,128)(2,1)S(1)} collective-permute-done((bf16[3,8,2048]{2,1,0:T(8,128)(2,1)S(1)}, bf16[3,8,2048]{2,1,0:T(8,128)(2,1)S(1)}, u32[]{:S(2)}, u32[]{:S(2)}) %collective-permute-start.4) | collective-permute-done | bytes 98336 | tf_op jit(solution)/shard_map/ppermute | solution.py:275
  10.0 1.5 %prompt.7 = bf16[3,8,2176]{2,1,0:T(8,128)(2,1)S(1)} custom-call(bf16[3,8,2048]{2,1,0:T(8,128)(2,1)S(1)} %collective-permute-done.4.q_ref, bf16[2048,256]{1,0:T(8,128)(2,1)S(1)} %get-tuple-element.23.k_ref, bf16[2048,256]{1,0:T(8,128)(2,1)S(1)} %get-tuple-element.24.v_ref), custom_call_target="tpu_custom_call" | custom-call | flops 402653184 | bytes 2097152 | tf_op jit(solution)/shard_map/prompt/pallas_call | solution.py:382
  11.6 3.8 %collective-permute-start.5 = (bf16[3,8,2176]{2,1,0:T(8,128)(2,1)S(1)}, bf16[3,8,2176]{2,1,0:T(8,128)(2,1)S(1)}, u32[]{:S(2)}, u32[]{:S(2)}) collective-permute-start(bf16[3,8,2176]{2,1,0:T(8,128)(2,1)S(1)} %prompt.7), channel_id=1, source_target_pairs={{0,12},{4,8},{8,4},{12,0},{1,13},{5,9},{9,5},{13,1},{2,14},{6,10},... | collective-permute-start | bytes 313352 | tf_op jit(solution)/shard_map/ppermute | solution.py:275
  15.4 0.4 collective-permute-done.2.q_ref
  15.8 1.5 %prompt.6 = bf16[3,8,2176]{2,1,0:T(8,128)(2,1)S(1)} custom-call(bf16[3,8,2048]{2,1,0:T(8,128)(2,1)S(1)} %collective-permute-done.2.q_ref, bf16[2048,256]{1,0:T(8,128)(2,1)S(1)} %get-tuple-element.23.k_ref, bf16[2048,256]{1,0:T(8,128)(2,1)S(1)} %get-tuple-element.24.v_ref), custom_call_target="tpu_custom_call" | custom-call | flops 402653184 | bytes 2097152 | tf_op jit(solution)/shard_map/prompt/pallas_call | solution.py:382
  17.3 1.3 %collective-permute-start.3 = (bf16[3,8,2176]{2,1,0:T(8,128)(2,1)S(1)}, bf16[3,8,2176]{2,1,0:T(8,128)(2,1)S(1)}, u32[]{:S(2)}, u32[]{:S(2)}) collective-permute-start(bf16[3,8,2176]{2,1,0:T(8,128)(2,1)S(1)} %prompt.6), channel_id=1, source_target_pairs={{0,8},{4,12},{8,0},{12,4},{1,9},{5,13},{9,1},{13,5},{2,10},{6,14},... | collective-permute-start | bytes 313352 | tf_op jit(solution)/shard_map/ppermute | solution.py:275
  18.6 0.0 collective-permute-done.q_ref
  18.6 0.0 slice-start
  18.6 1.5 %prompt.5 = bf16[3,8,2176]{2,1,0:T(8,128)(2,1)S(1)} custom-call(bf16[3,8,2048]{2,1,0:T(8,128)(2,1)S(1)} %collective-permute-done.q_ref, bf16[2048,256]{1,0:T(8,128)(2,1)S(1)} %get-tuple-element.23.k_ref, bf16[2048,256]{1,0:T(8,128)(2,1)S(1)} %get-tuple-element.24.v_ref), custom_call_target="tpu_custom_call" | custom-call | flops 402653184 | bytes 2097152 | tf_op jit(solution)/shard_map/prompt/pallas_call | solution.py:382
  20.2 1.3 %collective-permute-start.1 = (bf16[3,8,2176]{2,1,0:T(8,128)(2,1)S(1)}, bf16[3,8,2176]{2,1,0:T(8,128)(2,1)S(1)}, u32[]{:S(2)}, u32[]{:S(2)}) collective-permute-start(bf16[3,8,2176]{2,1,0:T(8,128)(2,1)S(1)} %prompt.5), channel_id=1, source_target_pairs={{0,4},{4,0},{8,12},{12,8},{1,5},{5,1},{9,13},{13,9},{2,6},{6,2},{1... | collective-permute-start | bytes 313352 | tf_op jit(solution)/shard_map/ppermute | solution.py:275
  21.4 0.0 slice-start.1
  21.4 3.7 %suffix.1 = (f32[3,16,2048]{2,1,0:T(8,128)S(1)}, f32[3,16,2048]{2,1,0:T(8,128)S(1)}) custom-call(bf16[3,16,2048]{2,1,0:T(8,128)(2,1)S(1)} %get-tuple-element.28.q_ref, s32[16]{0:T(128)} %len_hbm.1, bf16[16,256,256]{2,1,0:T(8,128)(2,1)} %k_hbm.1, bf16[16,256,256]{2,1,0:T(8,128)(2,1)} %v_hbm.1, bf16[3,16,256]{2,1,0:T(8,128)(2,1)} %bitcast.13, ...), custom_call_target="tpu_custom_call" | custom-call | flops 3000000000 | bytes 4194304 | tf_op jit(solution)/shard_map/suffix/pallas_call | solution.py:341
  25.1 1.5 %prompt.4.refs_1_ = bf16[3,8,2176]{2,1,0:T(8,128)(2,1)S(1)} custom-call(bf16[3,8,2048]{2,1,0:T(8,128)(2,1)S(1)} %get-tuple-element.22.q_ref, bf16[2048,256]{1,0:T(8,128)(2,1)S(1)} %get-tuple-element.23.k_ref, bf16[2048,256]{1,0:T(8,128)(2,1)S(1)} %get-tuple-element.24.v_ref), custom_call_target="tpu_custom_call" | custom-call | flops 402653184 | bytes 2097152 | tf_op jit(solution)/shard_map/prompt/pallas_call | solution.py:382
  26.6 0.0 collective-permute-done.5.refs_4_
  26.7 0.0 collective-permute-done.3.refs_3_
  26.7 0.0 collective-permute-done.1.refs_2_
  26.7 0.5 merge.1.own_ref
  27.2 2.1 %collective-permute-start.7 = (bf16[3,16,2048]{2,1,0:T(8,128)(2,1)S(1)}, bf16[3,16,2048]{2,1,0:T(8,128)(2,1)S(1)}, u32[]{:S(2)}, u32[]{:S(2)}) collective-permute-start(bf16[3,16,2048]{2,1,0:T(8,128)(2,1)S(1)} %merge.1.own_ref), channel_id=1, source_target_pairs={{0,8},{4,12},{8,0},{12,4},{1,9},{5,13},{9,1},{13,5},{2,10},{6,14},... | collective-permute-start | bytes 589832 | tf_op jit(solution)/shard_map/ppermute | solution.py:275
  29.2 0.5 collective-permute-start.6
  29.7 6.9 %collective-permute-done.7.g2_ref = bf16[3,16,2048]{2,1,0:T(8,128)(2,1)S(1)} collective-permute-done((bf16[3,16,2048]{2,1,0:T(8,128)(2,1)S(1)}, bf16[3,16,2048]{2,1,0:T(8,128)(2,1)S(1)}, u32[]{:S(2)}, u32[]{:S(2)}) %collective-permute-start.7) | collective-permute-done | bytes 196640 | tf_op jit(solution)/shard_map/ppermute | solution.py:275
  36.6 0.0 collective-permute-start.8
  36.6 0.3 collective-permute-done.6.g1_ref
  36.9 5.4 %collective-permute-done.8.g3_ref = bf16[3,16,2048]{2,1,0:T(8,128)(2,1)S(1)} collective-permute-done((bf16[3,16,2048]{2,1,0:T(8,128)(2,1)S(1)}, bf16[3,16,2048]{2,1,0:T(8,128)(2,1)S(1)}, u32[]{:S(2)}, u32[]{:S(2)}) %collective-permute-start.8) | collective-permute-done | bytes 196640 | tf_op jit(solution)/shard_map/ppermute | solution.py:275
  42.3 0.0 slice-done
  42.3 0.0 slice-done.1
  42.3 1.0 %shard_map.102 = (f32[3,16,1024]{2,1,0:T(8,128)S(1)}, f32[3,16,1024]{2,1,0:T(8,128)S(1)}, bf16[2,3,16,1024]{3,2,1,0:T(8,128)(2,1)S(1)}) custom-call(bf16[3,16,2048]{2,1,0:T(8,128)(2,1)S(1)} %merge.1.own_ref, bf16[3,16,2048]{2,1,0:T(8,128)(2,1)S(1)} %collective-permute-done.6.g1_ref, bf16[3,16,2048]{2,1,0:T(8,128)(2,1)S(1)} %collective-permute-done.7.g2_ref, ...), custom_call_target="tpu_custom_call" | custom-call | flops 805306368 | bytes 4194304 | tf_op jit(solution)/shard_map/pallas_call | solution.py:414
  43.3 0.1 collective-permute-start.11
  43.4 1.0 %shard_map.100 = (f32[3,16,1024]{2,1,0:T(8,128)S(1)}, f32[3,16,1024]{2,1,0:T(8,128)S(1)}, bf16[2,3,16,1024]{3,2,1,0:T(8,128)(2,1)S(1)}) custom-call(bf16[3,16,2048]{2,1,0:T(8,128)(2,1)S(1)} %merge.1.own_ref, bf16[3,16,2048]{2,1,0:T(8,128)(2,1)S(1)} %collective-permute-done.6.g1_ref, bf16[3,16,2048]{2,1,0:T(8,128)(2,1)S(1)} %collective-permute-done.7.g2_ref, ...), custom_call_target="tpu_custom_call" | custom-call | flops 805306368 | bytes 4194304 | tf_op jit(solution)/shard_map/pallas_call | solution.py:414
  44.4 0.6 %collective-permute-start.9 = (bf16[2,3,16,1024]{3,2,1,0:T(8,128)(2,1)S(1)}, bf16[2,3,16,1024]{3,2,1,0:T(8,128)(2,1)S(1)}, u32[]{:S(2)}, u32[]{:S(2)}) collective-permute-start(bf16[2,3,16,1024]{3,2,1,0:T(8,128)(2,1)S(1)} %get-tuple-element.32), channel_id=1, source_target_pairs={{0,1},{1,0},{2,3},{3,2},{4,5},{5,4},{6,7},{7,6},{8,9},{9,8},{10,11... | collective-permute-start | bytes 589832 | tf_op jit(solution)/shard_map/ppermute | solution.py:275
  45.0 0.0 collective-permute-done.11.got_ref.refs_4_
  45.0 1.5 %collective-permute-start.12 = (bf16[3,16,1024]{2,1,0:T(8,128)(2,1)S(1)}, bf16[3,16,1024]{2,1,0:T(8,128)(2,1)S(1)}, u32[]{:S(2)}, u32[]{:S(2)}) collective-permute-start(bf16[3,16,1024]{2,1,0:T(8,128)(2,1)S(1)} %shard_map.103), channel_id=1, source_target_pairs={{0,2},{1,3},{2,0},{3,1},{4,6},{5,7},{6,4},{7,5},{8,10},{9,11},{10,... | collective-permute-start | bytes 294920 | tf_op jit(solution)/shard_map/ppermute | solution.py:275
  46.5 0.0 collective-permute-done.9.got_ref.refs_1_
  46.6 1.0 %collective-permute-start.10 = (bf16[3,16,1024]{2,1,0:T(8,128)(2,1)S(1)}, bf16[3,16,1024]{2,1,0:T(8,128)(2,1)S(1)}, u32[]{:S(2)}, u32[]{:S(2)}) collective-permute-start(bf16[3,16,1024]{2,1,0:T(8,128)(2,1)S(1)} %shard_map.101), channel_id=1, source_target_pairs={{0,2},{1,3},{2,0},{3,1},{4,6},{5,7},{6,4},{7,5},{8,10},{9,11},{10,... | collective-permute-start | bytes 294920 | tf_op jit(solution)/shard_map/ppermute | solution.py:275
  47.6 2.9 %collective-permute-done.12.refs_5_ = bf16[3,16,1024]{2,1,0:T(8,128)(2,1)S(1)} collective-permute-done((bf16[3,16,1024]{2,1,0:T(8,128)(2,1)S(1)}, bf16[3,16,1024]{2,1,0:T(8,128)(2,1)S(1)}, u32[]{:S(2)}, u32[]{:S(2)}) %collective-permute-start.12) | collective-permute-done | bytes 98336 | tf_op jit(solution)/shard_map/ppermute | solution.py:275
  50.5 1.4 %collective-permute-done.10.refs_2_ = bf16[3,16,1024]{2,1,0:T(8,128)(2,1)S(1)} collective-permute-done((bf16[3,16,1024]{2,1,0:T(8,128)(2,1)S(1)}, bf16[3,16,1024]{2,1,0:T(8,128)(2,1)S(1)}, u32[]{:S(2)}, u32[]{:S(2)}) %collective-permute-start.10) | collective-permute-done | bytes 98336 | tf_op jit(solution)/shard_map/ppermute | solution.py:275
  51.9 0.7 %total.1 = bf16[3,16,2048]{2,1,0:T(8,128)(2,1)} custom-call(f32[3,16,1024]{2,1,0:T(8,128)S(1)} %get-tuple-element.31.refs_0_, bf16[2,3,16,1024]{3,2,1,0:T(8,128)(2,1)S(1)} %collective-permute-done.9.got_ref.refs_1_, bf16[3,16,1024]{2,1,0:T(8,128)(2,1)S(1)} %collective-permute-done.10.refs_2_, f32[3,16,1024]{2,1,0:T(8,128)S(1)} %get-tuple-element.34.refs_3_, ...), custom_call_target="tpu_custom_call" | custom-call | flops 98304 | bytes 1179648 | tf_op jit(solution)/shard_map/total/pallas_call | solution.py:449
  (3 shorter events, 0.0 us)
Async XLA Ops:
  1.2 8.8 %collective-permute-start.4 = (bf16[3,8,2048]{2,1,0:T(8,128)(2,1)S(1)}, bf16[3,8,2048]{2,1,0:T(8,128)(2,1)S(1)}, u32[]{:S(2)}, u32[]{:S(2)}) collective-permute-start(bf16[3,8,2048]{2,1,0:T(8,128)(2,1)S(1)} %get-tuple-element.27), channel_id=1, source_target_pairs={{0,12},{4,8},{8,4},{12,0},{1,13},{5,9},{9,5},{13,1},{2,14},{6,10},... | collective-permute-start | bytes 294920 | tf_op jit(solution)/shard_map/ppermute | solution.py:275
  6.3 9.5 %collective-permute-start.2 = (bf16[3,8,2048]{2,1,0:T(8,128)(2,1)S(1)}, bf16[3,8,2048]{2,1,0:T(8,128)(2,1)S(1)}, u32[]{:S(2)}, u32[]{:S(2)}) collective-permute-start(bf16[3,8,2048]{2,1,0:T(8,128)(2,1)S(1)} %get-tuple-element.26), channel_id=1, source_target_pairs={{0,8},{4,12},{8,0},{12,4},{1,9},{5,13},{9,1},{13,5},{2,10},{6,14},... | collective-permute-start | bytes 294920 | tf_op jit(solution)/shard_map/ppermute | solution.py:275
  6.3 12.3 %collective-permute-start = (bf16[3,8,2048]{2,1,0:T(8,128)(2,1)S(1)}, bf16[3,8,2048]{2,1,0:T(8,128)(2,1)S(1)}, u32[]{:S(2)}, u32[]{:S(2)}) collective-permute-start(bf16[3,8,2048]{2,1,0:T(8,128)(2,1)S(1)} %get-tuple-element.25), channel_id=1, source_target_pairs={{0,4},{4,0},{8,12},{12,8},{1,5},{5,1},{9,13},{13,9},{2,6},{6,2},{1... | collective-permute-start | bytes 294920 | tf_op jit(solution)/shard_map/ppermute | solution.py:275
  11.6 15.1 %collective-permute-start.5 = (bf16[3,8,2176]{2,1,0:T(8,128)(2,1)S(1)}, bf16[3,8,2176]{2,1,0:T(8,128)(2,1)S(1)}, u32[]{:S(2)}, u32[]{:S(2)}) collective-permute-start(bf16[3,8,2176]{2,1,0:T(8,128)(2,1)S(1)} %prompt.7), channel_id=1, source_target_pairs={{0,12},{4,8},{8,4},{12,0},{1,13},{5,9},{9,5},{13,1},{2,14},{6,10},... | collective-permute-start | bytes 313352 | tf_op jit(solution)/shard_map/ppermute | solution.py:275
  17.3 9.3 %collective-permute-start.3 = (bf16[3,8,2176]{2,1,0:T(8,128)(2,1)S(1)}, bf16[3,8,2176]{2,1,0:T(8,128)(2,1)S(1)}, u32[]{:S(2)}, u32[]{:S(2)}) collective-permute-start(bf16[3,8,2176]{2,1,0:T(8,128)(2,1)S(1)} %prompt.6), channel_id=1, source_target_pairs={{0,8},{4,12},{8,0},{12,4},{1,9},{5,13},{9,1},{13,5},{2,10},{6,14},... | collective-permute-start | bytes 313352 | tf_op jit(solution)/shard_map/ppermute | solution.py:275
  18.6 23.6 %slice-start = ((s8[8388608]{0:T(1024)(128)(4,1)}), s8[4194304]{0:T(1024)(128)(4,1)S(1)}, s32[]{:S(2)}) async-start(s8[8388608]{0:T(1024)(128)(4,1)} %bitcast.7), calls=%async_computation | async-start | bytes 8388608
  20.2 6.5 %collective-permute-start.1 = (bf16[3,8,2176]{2,1,0:T(8,128)(2,1)S(1)}, bf16[3,8,2176]{2,1,0:T(8,128)(2,1)S(1)}, u32[]{:S(2)}, u32[]{:S(2)}) collective-permute-start(bf16[3,8,2176]{2,1,0:T(8,128)(2,1)S(1)} %prompt.5), channel_id=1, source_target_pairs={{0,4},{4,0},{8,12},{12,8},{1,5},{5,1},{9,13},{13,9},{2,6},{6,2},{1... | collective-permute-start | bytes 313352 | tf_op jit(solution)/shard_map/ppermute | solution.py:275
  21.4 20.8 %slice-start.1 = ((s8[8388608]{0:T(1024)(128)(4,1)}), s8[4194304]{0:T(1024)(128)(4,1)S(1)}, s32[]{:S(2)}) async-start(s8[8388608]{0:T(1024)(128)(4,1)} %bitcast.7), calls=%async_computation.1 | async-start | bytes 8388608
  27.2 9.4 %collective-permute-start.7 = (bf16[3,16,2048]{2,1,0:T(8,128)(2,1)S(1)}, bf16[3,16,2048]{2,1,0:T(8,128)(2,1)S(1)}, u32[]{:S(2)}, u32[]{:S(2)}) collective-permute-start(bf16[3,16,2048]{2,1,0:T(8,128)(2,1)S(1)} %merge.1.own_ref), channel_id=1, source_target_pairs={{0,8},{4,12},{8,0},{12,4},{1,9},{5,13},{9,1},{13,5},{2,10},{6,14},... | collective-permute-start | bytes 589832 | tf_op jit(solution)/shard_map/ppermute | solution.py:275
  29.2 7.6 %collective-permute-start.6 = (bf16[3,16,2048]{2,1,0:T(8,128)(2,1)S(1)}, bf16[3,16,2048]{2,1,0:T(8,128)(2,1)S(1)}, u32[]{:S(2)}, u32[]{:S(2)}) collective-permute-start(bf16[3,16,2048]{2,1,0:T(8,128)(2,1)S(1)} %merge.1.own_ref), channel_id=1, source_target_pairs={{0,4},{4,0},{8,12},{12,8},{1,5},{5,1},{9,13},{13,9},{2,6},{6,2},{1... | collective-permute-start | bytes 589832 | tf_op jit(solution)/shard_map/ppermute | solution.py:275
  36.6 5.7 %collective-permute-start.8 = (bf16[3,16,2048]{2,1,0:T(8,128)(2,1)S(1)}, bf16[3,16,2048]{2,1,0:T(8,128)(2,1)S(1)}, u32[]{:S(2)}, u32[]{:S(2)}) collective-permute-start(bf16[3,16,2048]{2,1,0:T(8,128)(2,1)S(1)} %collective-permute-done.7.g2_ref), channel_id=1, source_target_pairs={{0,4},{4,0},{8,12},{12,8},{1,5},{5,1},{9,13},{13,9},{2,6},{6,2},{1... | collective-permute-start | bytes 589832 | tf_op jit(solution)/shard_map/ppermute | solution.py:275
  43.3 1.7 %collective-permute-start.11 = (bf16[2,3,16,1024]{3,2,1,0:T(8,128)(2,1)S(1)}, bf16[2,3,16,1024]{3,2,1,0:T(8,128)(2,1)S(1)}, u32[]{:S(2)}, u32[]{:S(2)}) collective-permute-start(bf16[2,3,16,1024]{3,2,1,0:T(8,128)(2,1)S(1)} %get-tuple-element.35), channel_id=1, source_target_pairs={{0,1},{1,0},{2,3},{3,2},{4,5},{5,4},{6,7},{7,6},{8,9},{9,8},{10,11... | collective-permute-start | bytes 589832 | tf_op jit(solution)/shard_map/ppermute | solution.py:275
  44.4 2.1 %collective-permute-start.9 = (bf16[2,3,16,1024]{3,2,1,0:T(8,128)(2,1)S(1)}, bf16[2,3,16,1024]{3,2,1,0:T(8,128)(2,1)S(1)}, u32[]{:S(2)}, u32[]{:S(2)}) collective-permute-start(bf16[2,3,16,1024]{3,2,1,0:T(8,128)(2,1)S(1)} %get-tuple-element.32), channel_id=1, source_target_pairs={{0,1},{1,0},{2,3},{3,2},{4,5},{5,4},{6,7},{7,6},{8,9},{9,8},{10,11... | collective-permute-start | bytes 589832 | tf_op jit(solution)/shard_map/ppermute | solution.py:275
  45.0 5.5 %collective-permute-start.12 = (bf16[3,16,1024]{2,1,0:T(8,128)(2,1)S(1)}, bf16[3,16,1024]{2,1,0:T(8,128)(2,1)S(1)}, u32[]{:S(2)}, u32[]{:S(2)}) collective-permute-start(bf16[3,16,1024]{2,1,0:T(8,128)(2,1)S(1)} %shard_map.103), channel_id=1, source_target_pairs={{0,2},{1,3},{2,0},{3,1},{4,6},{5,7},{6,4},{7,5},{8,10},{9,11},{10,... | collective-permute-start | bytes 294920 | tf_op jit(solution)/shard_map/ppermute | solution.py:275
  46.6 5.3 %collective-permute-start.10 = (bf16[3,16,1024]{2,1,0:T(8,128)(2,1)S(1)}, bf16[3,16,1024]{2,1,0:T(8,128)(2,1)S(1)}, u32[]{:S(2)}, u32[]{:S(2)}) collective-permute-start(bf16[3,16,1024]{2,1,0:T(8,128)(2,1)S(1)} %shard_map.101), channel_id=1, source_target_pairs={{0,2},{1,3},{2,0},{3,1},{4,6},{5,7},{6,4},{7,5},{8,10},{9,11},{10,... | collective-permute-start | bytes 294920 | tf_op jit(solution)/shard_map/ppermute | solution.py:275
where the time goes:
time: 52.8 us; the launch traced here: 52.6 us
  waiting for transfers between devices  18.7 us (35%)
  starting transfers between devices  18 us (34%)
  Pallas kernels  15.8 us (30%)
    ppermute x13, waiting for transfers between devices, swap(): return lax.ppermute(values, axis, pairs)  18.7 us
    ppermute x13, starting transfers between devices, swap(): return lax.ppermute(values, axis, pairs)  18 us
    pallas_call x4, Pallas kernels, local(): answers.append(prompt(asked, keys, values))  6.07 us
    pallas_call x1, Pallas kernels, local(): pl.pallas_call(functools.partial(suffix_kernel, group), out_shape=[jax.Sh...  3.68 us
    pallas_call x2, Pallas kernels, reduced(): pl.pallas_call(functools.partial(project_kernel, part * half), out_shape=...  2.05 us
    pallas_call x1, Pallas kernels, local(): pl.pallas_call(load_kernel, out_shape=[jax.ShapeDtypeStruct(prefix_keys.s...  1.57 us
    pallas_call x1, Pallas kernels, local(): pl.pallas_call(functools.partial(pack_kernel, capacity, direct), out_shap...  1.17 us
  transfers between devices with their start and end apart: 13, of which 7 were waited for; matrix products, arithmetic and copies ran while one was open for 0% of the time, Pallas kernels for 24%

commit v1 on v0

--- a/solution.py
+++ b/solution.py
@@ -16,7 +16,6 @@
 HIDDEN = -1e30
 MIB = 1 << 20
 PIECES = 4
-HALVES = 2
 NT = (((1,), (1,)), ((), ()))
 
 
@@ -187,9 +186,8 @@
     lane = lax.broadcasted_iota(jnp.int32, (size, LANES), 1)
     place = lax.rem(lane, all_heads)
     logs = [jnp.zeros((size, LANES), F32) for _ in range(steps)]
+    scores = []
     for h in range(heads):
-        keys = k_ref[:, pl.ds(h * HD, HD)]
-        values = v_ref[:, pl.ds(h * HD, HD)]
         q = jnp.concatenate(
             [
                 q_ref[s, :, pl.ds((h * group + g) * HD, HD)]
@@ -198,7 +196,11 @@
             ],
             0,
         )
-        score = lax.dot_general(q, keys, NT, preferred_element_type=F32)
+        keys = k_ref[:, pl.ds(h * HD, HD)]
+        scores.append(lax.dot_general(q, keys, NT, preferred_element_type=F32))
+    for h in range(heads):
+        values = v_ref[:, pl.ds(h * HD, HD)]
+        score = scores[h]
         peak = jnp.max(score, -1, keepdims=True)
         weight = jnp.exp2((score - peak) * to_two)
         total = jnp.sum(weight, -1, keepdims=True)
@@ -245,29 +247,65 @@
             out_ref[s, :, lanes] = mixed.astype(BF16)
 
 
-def project_kernel(first, own_ref, g1_ref, g2_ref, g3_ref, w_ref, own_out, far_out, beside_out, held):
+CHUNK = 512
+
+
+def early_kernel(own_ref, g1_ref, g2_ref, w_ref, own_out, far_out, beside_out, held):
     steps, count, _ = own_ref.shape
     each = steps * count
     me, mine = lax.axis_index("dp"), lax.axis_index("kv")
-    for shift, ref in enumerate((own_ref, g1_ref, g2_ref, g3_ref)):
+    for shift, ref in enumerate((own_ref, g1_ref, g2_ref)):
         place = (me ^ shift) ^ mine
         for s in range(steps):
             held[place, pl.ds(s * count, count), :] = ref[s]
+    held[(me ^ 3) ^ mine, :, :] = jnp.zeros(held.shape[1:], BF16)
     rows = held[...].reshape(4 * each, held.shape[2])
     outs = (own_out, beside_out.at[0], far_out, beside_out.at[1])
-    chunk = 512
-    for at in range(0, own_out.shape[2], chunk):
-        lanes = pl.ds(at, chunk)
-        product = jnp.dot(rows, w_ref[:, pl.ds(first + at, chunk)], preferred_element_type=F32)
+    for at in range(0, w_ref.shape[1], CHUNK):
+        lanes = pl.ds(at, CHUNK)
+        product = jnp.dot(rows, w_ref[:, lanes], preferred_element_type=F32)
         for part, ref in enumerate(outs):
             for s in range(steps):
                 row = part * each + s * count
                 ref[s, :, lanes] = product[row : row + count].astype(ref.dtype)
 
 
+def late_kernel(rows_ref, w_ref, keep_out, send_out, held):
+    steps, count, half = keep_out.shape
+    core = lax.axis_index("kv") & 1
+    for s in range(steps):
+        held[pl.ds(s * count, count), :] = rows_ref[s]
+    for which, ref in ((1, send_out), (0, keep_out)):
+        for at in range(0, half, CHUNK):
+            first = pl.multiple_of((core ^ which) * half + at, CHUNK)
+            product = jnp.dot(held[...], w_ref[:, pl.ds(first, CHUNK)], preferred_element_type=F32)
+            for s in range(steps):
+                ref[s, :, pl.ds(at, CHUNK)] = product[s * count : (s + 1) * count].astype(ref.dtype)
+
+
 def add_kernel(keep_ref, got_ref, send_ref):
     for s in range(keep_ref.shape[0]):
         send_ref[s] = (keep_ref[s] + got_ref[1, s].astype(F32)).astype(BF16)
+
+
+def late_add_kernel(keep_ref, got_ref, sum_ref, send_ref):
+    for s in range(keep_ref.shape[0]):
+        total = keep_ref[s] + got_ref[s].astype(F32)
+        sum_ref[s] = total
+        send_ref[s] = total.astype(BF16)
+
+
+def total_kernel(own_ref, got_ref, came_ref, half_ref, other_ref, out_ref):
+    steps, _, half = half_ref.shape
+    kv = lax.axis_index("kv")
+    here = kv == (lax.axis_index("dp") ^ 3)
+    for which, ref in ((0, half_ref), (1, other_ref)):
+        lanes = pl.ds(pl.multiple_of(((kv & 1) ^ which) * half, LANES), half)
+        for s in range(steps):
+            total = own_ref[s, :, lanes] + got_ref[0, s, :, lanes].astype(F32)
+            total = total + came_ref[s, :, lanes].astype(F32)
+            late = jnp.where(here, ref[s].astype(F32), 0.0)
+            out_ref[s, :, lanes] = (total + late).astype(BF16)
 
 
 def swap(values, axis, mask):
@@ -407,54 +445,43 @@
     by_two = swap(attended, "dp", 2)
     by_one = swap(attended, "dp", 1)
     by_three = swap(by_two, "dp", 1)
-    half = columns // HALVES
-    piece = (steps, count, half)
-
-    def reduced(part):
-        own_sum, far_sum, beside = pl.pallas_call(
-            functools.partial(project_kernel, part * half),
-            out_shape=[
-                jax.ShapeDtypeStruct(piece, F32),
-                jax.ShapeDtypeStruct(piece, F32),
-                jax.ShapeDtypeStruct((2, *piece), BF16),
-            ],
-            in_specs=[vmem] * 5,
-            out_specs=[vmem] * 3,
-            scratch_shapes=[pltpu.VMEM((owners, steps * count, width), BF16)],
+    half = columns // 2
+    piece, halved = (steps, count, columns), (steps, count, half)
+    flops = 2 * steps * count * width * columns
+
+    def call(kernel, shapes, operands, scratch=(), work=1 << 20):
+        return pl.pallas_call(
+            kernel,
+            out_shape=[jax.ShapeDtypeStruct(shape, kind) for shape, kind in shapes],
+            in_specs=[vmem] * len(operands),
+            out_specs=[vmem] * len(shapes),
+            scratch_shapes=list(scratch),
             compiler_params=params(8),
-            cost_estimate=cost(2 * owners * steps * count * width * half, width * half * 2),
-        )(attended, by_one, by_two, by_three, out_weight)
-        got = swap(beside, "kv", 1)
-        sent = pl.pallas_call(
-            add_kernel,
-            out_shape=jax.ShapeDtypeStruct(piece, BF16),
-            in_specs=[vmem] * 2,
-            out_specs=vmem,
-            compiler_params=params(4),
-            cost_estimate=cost(far_sum.size, far_sum.size * 12),
-        )(far_sum, got)
-        came = swap(sent, "kv", 2)
-        return own_sum, got, came
-
-    sums = [reduced(part) for part in range(HALVES)]
-
-    def total_kernel(*refs):
-        *in_refs, out_ref = refs
-        for part in range(HALVES):
-            own_ref, got_ref, came_ref = in_refs[3 * part : 3 * part + 3]
-            for s in range(steps):
-                total = own_ref[s] + got_ref[0, s].astype(F32) + came_ref[s].astype(F32)
-                out_ref[s, :, pl.ds(part * half, half)] = total.astype(BF16)
-
-    total = pl.pallas_call(
-        total_kernel,
-        out_shape=jax.ShapeDtypeStruct((steps, count, columns), BF16),
-        in_specs=[vmem] * (3 * HALVES),
-        out_specs=vmem,
-        compiler_params=params(8),
-        cost_estimate=cost(columns * count * steps, columns * count * steps * 12),
-        name="total",
-    )(*[value for part in sums for value in part])
+            cost_estimate=cost(work, 1 << 20),
+        )(*operands)
+
+    own_sum, far_sum, beside = call(
+        early_kernel,
+        [(piece, F32), (piece, F32), ((2, *piece), BF16)],
+        (attended, by_one, by_two, out_weight),
+        [pltpu.VMEM((owners, steps * count, width), BF16)],
+        4 * flops,
+    )
+    got = swap(beside, "kv", 1)
+    (sent,) = call(add_kernel, [(piece, BF16)], (far_sum, got))
+    came = swap(sent, "kv", 2)
+    keep, send = call(
+        late_kernel,
+        [(halved, F32), (halved, BF16)],
+        (by_three, out_weight),
+        [pltpu.VMEM((steps * count, width), BF16)],
+        flops,
+    )
+    sums = [(halved, F32), (halved, BF16)]
+    keep, send = call(late_add_kernel, sums, (keep, swap(send, "kv", 1)))
+    keep, send = call(late_add_kernel, sums, (keep, swap(send, "kv", 2)))
+    other = swap(send, "kv", 1)
+    (total,) = call(total_kernel, [(piece, BF16)], (own_sum, got, came, keep, other))
     return total.transpose(1, 0, 2)
 
 

time: 52.8 us -> 58.5 us (1.11)
  waiting for transfers between devices: 18.7 us -> 24.5 us
  starting transfers between devices: 18 us -> 17.2 us
  Pallas kernels: 15.8 us -> 16.5 us
    ppermute x13 -> x14, waiting for transfers between devices: 18.7 us -> 24.5 us  [swap(): return lax.ppermute(values, axis, pairs)]
    pallas_call x5 -> x6, Pallas kernels: 2.84 us -> 4.25 us  [call(): pl.pallas_call(kernel, out_shape=[jax.ShapeDtypeStruct(shape, kind) for s...]
    ppermute x13 -> x14, starting transfers between devices: 18 us -> 17.2 us  [swap(): return lax.ppermute(values, axis, pairs)]
    pallas_call x4, Pallas kernels: 6.07 us -> 5.34 us  [local(): answers.append(prompt(asked, keys, values))]
  transfers between devices with their start and end apart: 13 -> 14, of which waited for: 7 -> 9; matrix products, arithmetic and copies ran while one was open for 0% -> 0% of each run, Pallas kernels for 24% -> 21%
where the time goes in v1:
time: 58.5 us; the launch traced here: 58.3 us
  waiting for transfers between devices  24.5 us (42%)
  starting transfers between devices  17.2 us (29%)
  Pallas kernels  16.5 us (28%)
    ppermute x14, waiting for transfers between devices, swap(): return lax.ppermute(values, axis, pairs)  24.5 us
    ppermute x14, starting transfers between devices, swap(): return lax.ppermute(values, axis, pairs)  17.2 us
    pallas_call x4, Pallas kernels, local(): answers.append(prompt(asked, keys, values))  5.34 us
    pallas_call x6, Pallas kernels, call(): pl.pallas_call(kernel, out_shape=[jax.ShapeDtypeStruct(shape, kind) for s...  4.25 us
    pallas_call x1, Pallas kernels, local(): pl.pallas_call(functools.partial(suffix_kernel, group), out_shape=[jax.Sh...  3.68 us
    pallas_call x1, Pallas kernels, local(): pl.pallas_call(load_kernel, out_shape=[jax.ShapeDtypeStruct(prefix_keys.s...  1.57 us
    pallas_call x1, Pallas kernels, local(): pl.pallas_call(functools.partial(pack_kernel, capacity, direct), out_shap...  1.17 us
  transfers between devices with their start and end apart: 14, of which 9 were waited for; matrix products, arithmetic and copies ran while one was open for 0% of the time, Pallas kernels for 21%

profile of v1, /device:TPU:0, one launch (start us, length us, event | category | flops | bytes accessed | tf_op | source)
XLA Modules:
  0.0 58.3 jit_solution(3295684391302080372)
XLA Ops:
  0.0 1.2 %pack.1 = (bf16[3,16,2048]{2,1,0:T(8,128)(2,1)S(1)}, bf16[16,32]{1,0:T(8,128)(2,1)S(1)}, bf16[3,8,2048]{2,1,0:T(8,128)(2,1)S(1)}, bf16[3,8,2048]{2,1,0:T(8,128)(...) custom-call(s32[16]{0:T(128)} %bitcast.12, bf16[3,16,2048]{2,1,0:T(8,128)(2,1)} %bitcast.11), custom_call_target="tpu_custom_call" | custom-call | flops 6291456 | bytes 1048576 | tf_op jit(solution)/shard_map/pack/pallas_call | solution.py:341
  1.2 5.1 %collective-permute-start.4 = (bf16[3,8,2048]{2,1,0:T(8,128)(2,1)S(1)}, bf16[3,8,2048]{2,1,0:T(8,128)(2,1)S(1)}, u32[]{:S(2)}, u32[]{:S(2)}) collective-permute-start(bf16[3,8,2048]{2,1,0:T(8,128)(2,1)S(1)} %get-tuple-element.30), channel_id=1, source_target_pairs={{0,12},{4,8},{8,4},{12,0},{1,13},{5,9},{9,5},{13,1},{2,14},{6,10},... | collective-permute-start | bytes 294920 | tf_op jit(solution)/shard_map/ppermute | solution.py:313
  6.3 0.0 collective-permute-start.2
  6.3 0.6 %collective-permute-start = (bf16[3,8,2048]{2,1,0:T(8,128)(2,1)S(1)}, bf16[3,8,2048]{2,1,0:T(8,128)(2,1)S(1)}, u32[]{:S(2)}, u32[]{:S(2)}) collective-permute-start(bf16[3,8,2048]{2,1,0:T(8,128)(2,1)S(1)} %get-tuple-element.28), channel_id=1, source_target_pairs={{0,4},{4,0},{8,12},{12,8},{1,5},{5,1},{9,13},{13,9},{2,6},{6,2},{1... | collective-permute-start | bytes 294920 | tf_op jit(solution)/shard_map/ppermute | solution.py:313
  7.0 1.6 %load.1 = (bf16[2048,256]{1,0:T(8,128)(2,1)S(1)}, bf16[2048,256]{1,0:T(8,128)(2,1)S(1)}) custom-call(bf16[2048,256]{1,0:T(8,128)(2,1)} %bitcast.9, bf16[2048,256]{1,0:T(8,128)(2,1)} %bitcast.10), custom_call_target="tpu_custom_call" | custom-call | flops 500000000 | bytes 2097152 | tf_op jit(solution)/shard_map/load/pallas_call | solution.py:369
  8.5 1.5 %collective-permute-done.4.q_ref = bf16[3,8,2048]{2,1,0:T(8,128)(2,1)S(1)} collective-permute-done((bf16[3,8,2048]{2,1,0:T(8,128)(2,1)S(1)}, bf16[3,8,2048]{2,1,0:T(8,128)(2,1)S(1)}, u32[]{:S(2)}, u32[]{:S(2)}) %collective-permute-start.4) | collective-permute-done | bytes 98336 | tf_op jit(solution)/shard_map/ppermute | solution.py:313
  10.0 1.3 %prompt.7 = bf16[3,8,2176]{2,1,0:T(8,128)(2,1)S(1)} custom-call(bf16[3,8,2048]{2,1,0:T(8,128)(2,1)S(1)} %collective-permute-done.4.q_ref, bf16[2048,256]{1,0:T(8,128)(2,1)S(1)} %get-tuple-element.26.k_ref, bf16[2048,256]{1,0:T(8,128)(2,1)S(1)} %get-tuple-element.27.v_ref), custom_call_target="tpu_custom_call" | custom-call | flops 402653184 | bytes 2097152 | tf_op jit(solution)/shard_map/prompt/pallas_call | solution.py:420
  11.4 3.8 %collective-permute-start.5 = (bf16[3,8,2176]{2,1,0:T(8,128)(2,1)S(1)}, bf16[3,8,2176]{2,1,0:T(8,128)(2,1)S(1)}, u32[]{:S(2)}, u32[]{:S(2)}) collective-permute-start(bf16[3,8,2176]{2,1,0:T(8,128)(2,1)S(1)} %prompt.7), channel_id=1, source_target_pairs={{0,12},{4,8},{8,4},{12,0},{1,13},{5,9},{9,5},{13,1},{2,14},{6,10},... | collective-permute-start | bytes 313352 | tf_op jit(solution)/shard_map/ppermute | solution.py:313
  15.2 0.8 %collective-permute-done.2.q_ref = bf16[3,8,2048]{2,1,0:T(8,128)(2,1)S(1)} collective-permute-done((bf16[3,8,2048]{2,1,0:T(8,128)(2,1)S(1)}, bf16[3,8,2048]{2,1,0:T(8,128)(2,1)S(1)}, u32[]{:S(2)}, u32[]{:S(2)}) %collective-permute-start.2) | collective-permute-done | bytes 98336 | tf_op jit(solution)/shard_map/ppermute | solution.py:313
  16.0 1.3 %prompt.6 = bf16[3,8,2176]{2,1,0:T(8,128)(2,1)S(1)} custom-call(bf16[3,8,2048]{2,1,0:T(8,128)(2,1)S(1)} %collective-permute-done.2.q_ref, bf16[2048,256]{1,0:T(8,128)(2,1)S(1)} %get-tuple-element.26.k_ref, bf16[2048,256]{1,0:T(8,128)(2,1)S(1)} %get-tuple-element.27.v_ref), custom_call_target="tpu_custom_call" | custom-call | flops 402653184 | bytes 2097152 | tf_op jit(solution)/shard_map/prompt/pallas_call | solution.py:420
  17.3 1.0 %collective-permute-start.3 = (bf16[3,8,2176]{2,1,0:T(8,128)(2,1)S(1)}, bf16[3,8,2176]{2,1,0:T(8,128)(2,1)S(1)}, u32[]{:S(2)}, u32[]{:S(2)}) collective-permute-start(bf16[3,8,2176]{2,1,0:T(8,128)(2,1)S(1)} %prompt.6), channel_id=1, source_target_pairs={{0,8},{4,12},{8,0},{12,4},{1,9},{5,13},{9,1},{13,5},{2,10},{6,14},... | collective-permute-start | bytes 313352 | tf_op jit(solution)/shard_map/ppermute | solution.py:313
  18.3 0.0 collective-permute-done.q_ref
  18.3 0.0 slice-start
  18.3 1.3 %prompt.5 = bf16[3,8,2176]{2,1,0:T(8,128)(2,1)S(1)} custom-call(bf16[3,8,2048]{2,1,0:T(8,128)(2,1)S(1)} %collective-permute-done.q_ref, bf16[2048,256]{1,0:T(8,128)(2,1)S(1)} %get-tuple-element.26.k_ref, bf16[2048,256]{1,0:T(8,128)(2,1)S(1)} %get-tuple-element.27.v_ref), custom_call_target="tpu_custom_call" | custom-call | flops 402653184 | bytes 2097152 | tf_op jit(solution)/shard_map/prompt/pallas_call | solution.py:420
  19.6 2.7 %collective-permute-start.1 = (bf16[3,8,2176]{2,1,0:T(8,128)(2,1)S(1)}, bf16[3,8,2176]{2,1,0:T(8,128)(2,1)S(1)}, u32[]{:S(2)}, u32[]{:S(2)}) collective-permute-start(bf16[3,8,2176]{2,1,0:T(8,128)(2,1)S(1)} %prompt.5), channel_id=1, source_target_pairs={{0,4},{4,0},{8,12},{12,8},{1,5},{5,1},{9,13},{13,9},{2,6},{6,2},{1... | collective-permute-start | bytes 313352 | tf_op jit(solution)/shard_map/ppermute | solution.py:313
  22.3 0.0 slice-start.1
  22.3 3.7 %suffix.1 = (f32[3,16,2048]{2,1,0:T(8,128)S(1)}, f32[3,16,2048]{2,1,0:T(8,128)S(1)}) custom-call(bf16[3,16,2048]{2,1,0:T(8,128)(2,1)S(1)} %get-tuple-element.31.q_ref, s32[16]{0:T(128)} %len_hbm.1, bf16[16,256,256]{2,1,0:T(8,128)(2,1)} %k_hbm.1, bf16[16,256,256]{2,1,0:T(8,128)(2,1)} %v_hbm.1, bf16[3,16,256]{2,1,0:T(8,128)(2,1)} %bitcast.13, ...), custom_call_target="tpu_custom_call" | custom-call | flops 3000000000 | bytes 4194304 | tf_op jit(solution)/shard_map/suffix/pallas_call | solution.py:379
  26.0 1.3 %prompt.4.refs_1_ = bf16[3,8,2176]{2,1,0:T(8,128)(2,1)S(1)} custom-call(bf16[3,8,2048]{2,1,0:T(8,128)(2,1)S(1)} %get-tuple-element.25.q_ref, bf16[2048,256]{1,0:T(8,128)(2,1)S(1)} %get-tuple-element.26.k_ref, bf16[2048,256]{1,0:T(8,128)(2,1)S(1)} %get-tuple-element.27.v_ref), custom_call_target="tpu_custom_call" | custom-call | flops 402653184 | bytes 2097152 | tf_op jit(solution)/shard_map/prompt/pallas_call | solution.py:420
  27.4 0.0 collective-permute-done.5.refs_4_
  27.4 0.0 collective-permute-done.3.refs_3_
  27.4 0.0 collective-permute-done.1.refs_2_
  27.4 0.5 merge.1.own_ref
  27.9 0.6 %collective-permute-start.7 = (bf16[3,16,2048]{2,1,0:T(8,128)(2,1)S(1)}, bf16[3,16,2048]{2,1,0:T(8,128)(2,1)S(1)}, u32[]{:S(2)}, u32[]{:S(2)}) collective-permute-start(bf16[3,16,2048]{2,1,0:T(8,128)(2,1)S(1)} %merge.1.own_ref), channel_id=1, source_target_pairs={{0,8},{4,12},{8,0},{12,4},{1,9},{5,13},{9,1},{13,5},{2,10},{6,14},... | collective-permute-start | bytes 589832 | tf_op jit(solution)/shard_map/ppermute | solution.py:313
  28.5 0.9 %collective-permute-start.6 = (bf16[3,16,2048]{2,1,0:T(8,128)(2,1)S(1)}, bf16[3,16,2048]{2,1,0:T(8,128)(2,1)S(1)}, u32[]{:S(2)}, u32[]{:S(2)}) collective-permute-start(bf16[3,16,2048]{2,1,0:T(8,128)(2,1)S(1)} %merge.1.own_ref), channel_id=1, source_target_pairs={{0,4},{4,0},{8,12},{12,8},{1,5},{5,1},{9,13},{13,9},{2,6},{6,2},{1... | collective-permute-start | bytes 589832 | tf_op jit(solution)/shard_map/ppermute | solution.py:313
  29.4 6.8 %collective-permute-done.7.g2_ref = bf16[3,16,2048]{2,1,0:T(8,128)(2,1)S(1)} collective-permute-done((bf16[3,16,2048]{2,1,0:T(8,128)(2,1)S(1)}, bf16[3,16,2048]{2,1,0:T(8,128)(2,1)S(1)}, u32[]{:S(2)}, u32[]{:S(2)}) %collective-permute-start.7) | collective-permute-done | bytes 196640 | tf_op jit(solution)/shard_map/ppermute | solution.py:313
  36.2 0.1 collective-permute-done.6.g1_ref
  36.3 0.0 slice-done
  36.3 0.0 slice-done.1
  36.3 1.8 %shard_map.100 = (f32[3,16,2048]{2,1,0:T(8,128)S(1)}, f32[3,16,2048]{2,1,0:T(8,128)S(1)}, bf16[2,3,16,2048]{3,2,1,0:T(8,128)(2,1)S(1)}) custom-call(bf16[3,16,2048]{2,1,0:T(8,128)(2,1)S(1)} %merge.1.own_ref, bf16[3,16,2048]{2,1,0:T(8,128)(2,1)S(1)} %collective-permute-done.6.g1_ref, bf16[3,16,2048]{2,1,0:T(8,128)(2,1)S(1)} %collective-permute-done.7.g2_ref, ...), custom_call_target="tpu_custom_call" | custom-call | flops 1610612736 | bytes 1048576 | tf_op jit(solution)/shard_map/pallas_call | solution.py:453
  38.1 0.1 collective-permute-start.8
  38.2 0.1 collective-permute-start.10
  38.3 7.2 %collective-permute-done.10.rows_ref = bf16[3,16,2048]{2,1,0:T(8,128)(2,1)S(1)} collective-permute-done((bf16[3,16,2048]{2,1,0:T(8,128)(2,1)S(1)}, bf16[3,16,2048]{2,1,0:T(8,128)(2,1)S(1)}, u32[]{:S(2)}, u32[]{:S(2)}) %collective-permute-start.10) | collective-permute-done | bytes 196640 | tf_op jit(solution)/shard_map/ppermute | solution.py:313
  45.5 1.5 %shard_map.102 = (f32[3,16,1024]{2,1,0:T(8,128)S(1)}, bf16[3,16,1024]{2,1,0:T(8,128)(2,1)S(1)}) custom-call(bf16[3,16,2048]{2,1,0:T(8,128)(2,1)S(1)} %collective-permute-done.10.rows_ref, bf16[2048,2048]{1,0:T(8,128)(2,1)S(1)} %bitcast.8), custom_call_target="tpu_custom_call" | custom-call | flops 402653184 | bytes 1048576 | tf_op jit(solution)/shard_map/pallas_call | solution.py:453
  47.0 0.0 collective-permute-start.11
  47.1 1.3 %collective-permute-done.11.got_ref = bf16[3,16,1024]{2,1,0:T(8,128)(2,1)S(1)} collective-permute-done((bf16[3,16,1024]{2,1,0:T(8,128)(2,1)S(1)}, bf16[3,16,1024]{2,1,0:T(8,128)(2,1)S(1)}, u32[]{:S(2)}, u32[]{:S(2)}) %collective-permute-start.11) | collective-permute-done | bytes 98336 | tf_op jit(solution)/shard_map/ppermute | solution.py:313
  48.4 1.6 %collective-permute-start.12 = (bf16[3,16,1024]{2,1,0:T(8,128)(2,1)S(1)}, bf16[3,16,1024]{2,1,0:T(8,128)(2,1)S(1)}, u32[]{:S(2)}, u32[]{:S(2)}) collective-permute-start(bf16[3,16,1024]{2,1,0:T(8,128)(2,1)S(1)} %get-tuple-element.40), channel_id=1, source_target_pairs={{0,2},{1,3},{2,0},{3,1},{4,6},{5,7},{6,4},{7,5},{8,10},{9,11},{10,... | collective-permute-start | bytes 294920 | tf_op jit(solution)/shard_map/ppermute | solution.py:313
  50.0 0.0 collective-permute-done.8.got_ref
  50.0 0.6 %collective-permute-start.9 = (bf16[3,16,2048]{2,1,0:T(8,128)(2,1)S(1)}, bf16[3,16,2048]{2,1,0:T(8,128)(2,1)S(1)}, u32[]{:S(2)}, u32[]{:S(2)}) collective-permute-start(bf16[3,16,2048]{2,1,0:T(8,128)(2,1)S(1)} %shard_map.101), channel_id=1, source_target_pairs={{0,2},{1,3},{2,0},{3,1},{4,6},{5,7},{6,4},{7,5},{8,10},{9,11},{10,... | collective-permute-start | bytes 589832 | tf_op jit(solution)/shard_map/ppermute | solution.py:313
  50.6 3.5 %collective-permute-done.12.got_ref = bf16[3,16,1024]{2,1,0:T(8,128)(2,1)S(1)} collective-permute-done((bf16[3,16,1024]{2,1,0:T(8,128)(2,1)S(1)}, bf16[3,16,1024]{2,1,0:T(8,128)(2,1)S(1)}, u32[]{:S(2)}, u32[]{:S(2)}) %collective-permute-start.12) | collective-permute-done | bytes 98336 | tf_op jit(solution)/shard_map/ppermute | solution.py:313
  54.1 0.1 collective-permute-start.13
  54.2 1.3 %collective-permute-done.13.other_ref = bf16[3,16,1024]{2,1,0:T(8,128)(2,1)S(1)} collective-permute-done((bf16[3,16,1024]{2,1,0:T(8,128)(2,1)S(1)}, bf16[3,16,1024]{2,1,0:T(8,128)(2,1)S(1)}, u32[]{:S(2)}, u32[]{:S(2)}) %collective-permute-start.13) | collective-permute-done | bytes 98336 | tf_op jit(solution)/shard_map/ppermute | solution.py:313
  55.5 2.0 %collective-permute-done.9.came_ref = bf16[3,16,2048]{2,1,0:T(8,128)(2,1)S(1)} collective-permute-done((bf16[3,16,2048]{2,1,0:T(8,128)(2,1)S(1)}, bf16[3,16,2048]{2,1,0:T(8,128)(2,1)S(1)}, u32[]{:S(2)}, u32[]{:S(2)}) %collective-permute-start.9) | collective-permute-done | bytes 196640 | tf_op jit(solution)/shard_map/ppermute | solution.py:313
  57.5 0.8 %shard_map.105 = bf16[3,16,2048]{2,1,0:T(8,128)(2,1)} custom-call(f32[3,16,2048]{2,1,0:T(8,128)S(1)} %get-tuple-element.34.own_ref, bf16[2,3,16,2048]{3,2,1,0:T(8,128)(2,1)S(1)} %collective-permute-done.8.got_ref, bf16[3,16,2048]{2,1,0:T(8,128)(2,1)S(1)} %collective-permute-done.9.came_ref, f32[3,16,1024]{2,1,0:T(8,128)S(1)} %get-tuple-element.41.half_ref, ...), custom_call_target="tpu_custom_call" | custom-call | flops 1048576 | bytes 1048576 | tf_op jit(solution)/shard_map/pallas_call | solution.py:453
  (4 shorter events, 0.1 us)
Async XLA Ops:
  1.2 8.8 %collective-permute-start.4 = (bf16[3,8,2048]{2,1,0:T(8,128)(2,1)S(1)}, bf16[3,8,2048]{2,1,0:T(8,128)(2,1)S(1)}, u32[]{:S(2)}, u32[]{:S(2)}) collective-permute-start(bf16[3,8,2048]{2,1,0:T(8,128)(2,1)S(1)} %get-tuple-element.30), channel_id=1, source_target_pairs={{0,12},{4,8},{8,4},{12,0},{1,13},{5,9},{9,5},{13,1},{2,14},{6,10},... | collective-permute-start | bytes 294920 | tf_op jit(solution)/shard_map/ppermute | solution.py:313
  6.3 9.6 %collective-permute-start.2 = (bf16[3,8,2048]{2,1,0:T(8,128)(2,1)S(1)}, bf16[3,8,2048]{2,1,0:T(8,128)(2,1)S(1)}, u32[]{:S(2)}, u32[]{:S(2)}) collective-permute-start(bf16[3,8,2048]{2,1,0:T(8,128)(2,1)S(1)} %get-tuple-element.29), channel_id=1, source_target_pairs={{0,8},{4,12},{8,0},{12,4},{1,9},{5,13},{9,1},{13,5},{2,10},{6,14},... | collective-permute-start | bytes 294920 | tf_op jit(solution)/shard_map/ppermute | solution.py:313
  6.3 11.9 %collective-permute-start = (bf16[3,8,2048]{2,1,0:T(8,128)(2,1)S(1)}, bf16[3,8,2048]{2,1,0:T(8,128)(2,1)S(1)}, u32[]{:S(2)}, u32[]{:S(2)}) collective-permute-start(bf16[3,8,2048]{2,1,0:T(8,128)(2,1)S(1)} %get-tuple-element.28), channel_id=1, source_target_pairs={{0,4},{4,0},{8,12},{12,8},{1,5},{5,1},{9,13},{13,9},{2,6},{6,2},{1... | collective-permute-start | bytes 294920 | tf_op jit(solution)/shard_map/ppermute | solution.py:313
  11.4 16.0 %collective-permute-start.5 = (bf16[3,8,2176]{2,1,0:T(8,128)(2,1)S(1)}, bf16[3,8,2176]{2,1,0:T(8,128)(2,1)S(1)}, u32[]{:S(2)}, u32[]{:S(2)}) collective-permute-start(bf16[3,8,2176]{2,1,0:T(8,128)(2,1)S(1)} %prompt.7), channel_id=1, source_target_pairs={{0,12},{4,8},{8,4},{12,0},{1,13},{5,9},{9,5},{13,1},{2,14},{6,10},... | collective-permute-start | bytes 313352 | tf_op jit(solution)/shard_map/ppermute | solution.py:313
  17.3 10.1 %collective-permute-start.3 = (bf16[3,8,2176]{2,1,0:T(8,128)(2,1)S(1)}, bf16[3,8,2176]{2,1,0:T(8,128)(2,1)S(1)}, u32[]{:S(2)}, u32[]{:S(2)}) collective-permute-start(bf16[3,8,2176]{2,1,0:T(8,128)(2,1)S(1)} %prompt.6), channel_id=1, source_target_pairs={{0,8},{4,12},{8,0},{12,4},{1,9},{5,13},{9,1},{13,5},{2,10},{6,14},... | collective-permute-start | bytes 313352 | tf_op jit(solution)/shard_map/ppermute | solution.py:313
  18.3 18.0 %slice-start = ((s8[8388608]{0:T(1024)(128)(4,1)}), s8[4194304]{0:T(1024)(128)(4,1)S(1)}, s32[]{:S(2)}) async-start(s8[8388608]{0:T(1024)(128)(4,1)} %bitcast.7), calls=%async_computation | async-start | bytes 8388608
  19.6 7.8 %collective-permute-start.1 = (bf16[3,8,2176]{2,1,0:T(8,128)(2,1)S(1)}, bf16[3,8,2176]{2,1,0:T(8,128)(2,1)S(1)}, u32[]{:S(2)}, u32[]{:S(2)}) collective-permute-start(bf16[3,8,2176]{2,1,0:T(8,128)(2,1)S(1)} %prompt.5), channel_id=1, source_target_pairs={{0,4},{4,0},{8,12},{12,8},{1,5},{5,1},{9,13},{13,9},{2,6},{6,2},{1... | collective-permute-start | bytes 313352 | tf_op jit(solution)/shard_map/ppermute | solution.py:313
  22.3 13.9 %slice-start.1 = ((s8[8388608]{0:T(1024)(128)(4,1)}), s8[4194304]{0:T(1024)(128)(4,1)S(1)}, s32[]{:S(2)}) async-start(s8[8388608]{0:T(1024)(128)(4,1)} %bitcast.7), calls=%async_computation.1 | async-start | bytes 8388608
  27.9 8.3 %collective-permute-start.7 = (bf16[3,16,2048]{2,1,0:T(8,128)(2,1)S(1)}, bf16[3,16,2048]{2,1,0:T(8,128)(2,1)S(1)}, u32[]{:S(2)}, u32[]{:S(2)}) collective-permute-start(bf16[3,16,2048]{2,1,0:T(8,128)(2,1)S(1)} %merge.1.own_ref), channel_id=1, source_target_pairs={{0,8},{4,12},{8,0},{12,4},{1,9},{5,13},{9,1},{13,5},{2,10},{6,14},... | collective-permute-start | bytes 589832 | tf_op jit(solution)/shard_map/ppermute | solution.py:313
  28.5 7.8 %collective-permute-start.6 = (bf16[3,16,2048]{2,1,0:T(8,128)(2,1)S(1)}, bf16[3,16,2048]{2,1,0:T(8,128)(2,1)S(1)}, u32[]{:S(2)}, u32[]{:S(2)}) collective-permute-start(bf16[3,16,2048]{2,1,0:T(8,128)(2,1)S(1)} %merge.1.own_ref), channel_id=1, source_target_pairs={{0,4},{4,0},{8,12},{12,8},{1,5},{5,1},{9,13},{13,9},{2,6},{6,2},{1... | collective-permute-start | bytes 589832 | tf_op jit(solution)/shard_map/ppermute | solution.py:313
  38.1 11.8 %collective-permute-start.8 = (bf16[2,3,16,2048]{3,2,1,0:T(8,128)(2,1)S(1)}, bf16[2,3,16,2048]{3,2,1,0:T(8,128)(2,1)S(1)}, u32[]{:S(2)}, u32[]{:S(2)}) collective-permute-start(bf16[2,3,16,2048]{3,2,1,0:T(8,128)(2,1)S(1)} %get-tuple-element.35), channel_id=1, source_target_pairs={{0,1},{1,0},{2,3},{3,2},{4,5},{5,4},{6,7},{7,6},{8,9},{9,8},{10,11... | collective-permute-start | bytes 1179656 | tf_op jit(solution)/shard_map/ppermute | solution.py:313
  38.2 7.3 %collective-permute-start.10 = (bf16[3,16,2048]{2,1,0:T(8,128)(2,1)S(1)}, bf16[3,16,2048]{2,1,0:T(8,128)(2,1)S(1)}, u32[]{:S(2)}, u32[]{:S(2)}) collective-permute-start(bf16[3,16,2048]{2,1,0:T(8,128)(2,1)S(1)} %collective-permute-done.7.g2_ref), channel_id=1, source_target_pairs={{0,4},{4,0},{8,12},{12,8},{1,5},{5,1},{9,13},{13,9},{2,6},{6,2},{1... | collective-permute-start | bytes 589832 | tf_op jit(solution)/shard_map/ppermute | solution.py:313
  47.0 1.3 %collective-permute-start.11 = (bf16[3,16,1024]{2,1,0:T(8,128)(2,1)S(1)}, bf16[3,16,1024]{2,1,0:T(8,128)(2,1)S(1)}, u32[]{:S(2)}, u32[]{:S(2)}) collective-permute-start(bf16[3,16,1024]{2,1,0:T(8,128)(2,1)S(1)} %get-tuple-element.38), channel_id=1, source_target_pairs={{0,1},{1,0},{2,3},{3,2},{4,5},{5,4},{6,7},{7,6},{8,9},{9,8},{10,11... | collective-permute-start | bytes 294920 | tf_op jit(solution)/shard_map/ppermute | solution.py:313
  48.4 5.7 %collective-permute-start.12 = (bf16[3,16,1024]{2,1,0:T(8,128)(2,1)S(1)}, bf16[3,16,1024]{2,1,0:T(8,128)(2,1)S(1)}, u32[]{:S(2)}, u32[]{:S(2)}) collective-permute-start(bf16[3,16,1024]{2,1,0:T(8,128)(2,1)S(1)} %get-tuple-element.40), channel_id=1, source_target_pairs={{0,2},{1,3},{2,0},{3,1},{4,6},{5,7},{6,4},{7,5},{8,10},{9,11},{10,... | collective-permute-start | bytes 294920 | tf_op jit(solution)/shard_map/ppermute | solution.py:313
  50.0 7.5 %collective-permute-start.9 = (bf16[3,16,2048]{2,1,0:T(8,128)(2,1)S(1)}, bf16[3,16,2048]{2,1,0:T(8,128)(2,1)S(1)}, u32[]{:S(2)}, u32[]{:S(2)}) collective-permute-start(bf16[3,16,2048]{2,1,0:T(8,128)(2,1)S(1)} %shard_map.101), channel_id=1, source_target_pairs={{0,2},{1,3},{2,0},{3,1},{4,6},{5,7},{6,4},{7,5},{8,10},{9,11},{10,... | collective-permute-start | bytes 589832 | tf_op jit(solution)/shard_map/ppermute | solution.py:313
  54.1 1.4 %collective-permute-start.13 = (bf16[3,16,1024]{2,1,0:T(8,128)(2,1)S(1)}, bf16[3,16,1024]{2,1,0:T(8,128)(2,1)S(1)}, u32[]{:S(2)}, u32[]{:S(2)}) collective-permute-start(bf16[3,16,1024]{2,1,0:T(8,128)(2,1)S(1)} %get-tuple-element.42), channel_id=1, source_target_pairs={{0,1},{1,0},{2,3},{3,2},{4,5},{5,4},{6,7},{7,6},{8,9},{9,8},{10,11... | collective-permute-start | bytes 294920 | tf_op jit(solution)/shard_map/ppermute | solution.py:313

commit v2 on v1

--- a/solution.py
+++ b/solution.py
@@ -184,8 +184,8 @@
     scale = 1.0 / math.sqrt(HD)
     to_two = scale * math.log2(math.e)
     lane = lax.broadcasted_iota(jnp.int32, (size, LANES), 1)
-    place = lax.rem(lane, all_heads)
-    logs = [jnp.zeros((size, LANES), F32) for _ in range(steps)]
+    place = lax.rem(lane, all_heads) + lax.div(lane, 2 * all_heads) * all_heads
+    logs = jnp.zeros((size, LANES), F32)
     scores = []
     for h in range(heads):
         q = jnp.concatenate(
@@ -209,16 +209,12 @@
         for s in range(steps):
             for g in range(group):
                 at = (s * group + g) * size
-                lanes = pl.ds((h * group + g) * HD, HD)
-                out_ref[s, :, lanes] = out[at : at + size].astype(BF16)
-                logs[s] = jnp.where(place == h * group + g, log_total[at : at + size], logs[s])
-    for s in range(steps):
-        high = logs[s].astype(BF16).astype(F32)
-        rest = logs[s] - high
-        middle = rest.astype(BF16).astype(F32)
-        low = rest - middle
-        terms = jnp.where(lane < all_heads, high, jnp.where(lane < 2 * all_heads, middle, low))
-        out_ref[s, :, pl.ds(width, LANES)] = terms.astype(BF16)
+                head = s * all_heads + h * group + g
+                out_ref[:, pl.ds(head * HD, HD)] = out[at : at + size].astype(BF16)
+                logs = jnp.where(place == head, log_total[at : at + size], logs)
+    high = logs.astype(BF16).astype(F32)
+    terms = jnp.where(lax.rem(lane, 2 * all_heads) < all_heads, high, logs - high)
+    out_ref[:, pl.ds(steps * width, LANES)] = terms.astype(BF16)
 
 
 def merge_kernel(blocks, *refs):
@@ -227,15 +223,12 @@
     steps, count, width = own_ref.shape
     all_heads = width // HD
     choice = choice_ref[...]
+    received = jnp.concatenate([ref[...] for ref in row_refs], 0)
+    received = jnp.dot(choice, received, preferred_element_type=F32)
     for s in range(steps):
-        rows = jnp.concatenate([ref[s] for ref in row_refs], 0)
-        rows = jnp.dot(choice, rows, preferred_element_type=F32)
-        terms = rows[:, width:]
-        logs = (
-            terms[:, :all_heads]
-            + terms[:, all_heads : 2 * all_heads]
-            + terms[:, 2 * all_heads : 3 * all_heads]
-        )
+        rows = received[:, s * width : (s + 1) * width]
+        at = steps * width + 2 * s * all_heads
+        logs = received[:, at : at + all_heads] + received[:, at + all_heads : at + 2 * all_heads]
         for h in range(all_heads):
             lanes = slice(h * HD, (h + 1) * HD)
             first = jnp.broadcast_to(logs[:, h : h + 1], (count, HD))
@@ -408,7 +401,7 @@
 
     prompt = pl.pallas_call(
         functools.partial(prompt_kernel, group),
-        out_shape=jax.ShapeDtypeStruct((steps, size, width + LANES), BF16),
+        out_shape=jax.ShapeDtypeStruct((size, steps * width + LANES), BF16),
         in_specs=[vmem] * 3,
         out_specs=vmem,
         compiler_params=params(12 if direct else 48),
@@ -421,7 +414,9 @@
     if direct:
         home = [answers[0]] + [swap(answers[i], "dp", i) for i in (1, 2, 3)]
     else:
-        home = [all_to_all(answers[0])]
+        moved = answers[0].reshape(owners, capacity, -1)
+        moved = lax.all_to_all(moved, "dp", split_axis=0, concat_axis=0, tiled=True)
+        home = [moved.reshape(owners * capacity, -1)]
 
     attended = pl.pallas_call(
         functools.partial(merge_kernel, blocks),

time: 58.5 us -> 58.4 us (level)
  no operation moved by 1% of the time
where the time goes in v2:
time: 58.4 us; the launch traced here: 58.2 us
  waiting for transfers between devices  24.5 us (42%)
  starting transfers between devices  17.2 us (29%)
  Pallas kernels  16.4 us (28%)
    ppermute x14, waiting for transfers between devices, swap(): return lax.ppermute(values, axis, pairs)  24.5 us
    ppermute x14, starting transfers between devices, swap(): return lax.ppermute(values, axis, pairs)  17.2 us
    pallas_call x4, Pallas kernels, local(): answers.append(prompt(asked, keys, values))  5.25 us
    pallas_call x6, Pallas kernels, call(): pl.pallas_call(kernel, out_shape=[jax.ShapeDtypeStruct(shape, kind) for s...  4.24 us
    pallas_call x1, Pallas kernels, local(): pl.pallas_call(functools.partial(suffix_kernel, group), out_shape=[jax.Sh...  3.68 us
    pallas_call x1, Pallas kernels, local(): pl.pallas_call(load_kernel, out_shape=[jax.ShapeDtypeStruct(prefix_keys.s...  1.57 us
    pallas_call x1, Pallas kernels, local(): pl.pallas_call(functools.partial(pack_kernel, capacity, direct), out_shap...  1.17 us
  transfers between devices with their start and end apart: 14, of which 9 were waited for; matrix products, arithmetic and copies ran while one was open for 0% of the time, Pallas kernels for 21%

profile of v2, /device:TPU:0, one launch (start us, length us, event | category | flops | bytes accessed | tf_op | source)
XLA Modules:
  0.0 58.2 jit_solution(13669396562336713174)
XLA Ops:
  0.0 1.2 %pack.1 = (bf16[3,16,2048]{2,1,0:T(8,128)(2,1)S(1)}, bf16[16,32]{1,0:T(8,128)(2,1)S(1)}, bf16[3,8,2048]{2,1,0:T(8,128)(2,1)S(1)}, bf16[3,8,2048]{2,1,0:T(8,128)(...) custom-call(s32[16]{0:T(128)} %bitcast.12, bf16[3,16,2048]{2,1,0:T(8,128)(2,1)} %bitcast.11), custom_call_target="tpu_custom_call" | custom-call | flops 6291456 | bytes 1048576 | tf_op jit(solution)/shard_map/pack/pallas_call | solution.py:334
  1.2 5.1 %collective-permute-start.4 = (bf16[3,8,2048]{2,1,0:T(8,128)(2,1)S(1)}, bf16[3,8,2048]{2,1,0:T(8,128)(2,1)S(1)}, u32[]{:S(2)}, u32[]{:S(2)}) collective-permute-start(bf16[3,8,2048]{2,1,0:T(8,128)(2,1)S(1)} %get-tuple-element.30), channel_id=1, source_target_pairs={{0,12},{4,8},{8,4},{12,0},{1,13},{5,9},{9,5},{13,1},{2,14},{6,10},... | collective-permute-start | bytes 294920 | tf_op jit(solution)/shard_map/ppermute | solution.py:306
  6.3 0.0 collective-permute-start.2
  6.3 0.6 %collective-permute-start = (bf16[3,8,2048]{2,1,0:T(8,128)(2,1)S(1)}, bf16[3,8,2048]{2,1,0:T(8,128)(2,1)S(1)}, u32[]{:S(2)}, u32[]{:S(2)}) collective-permute-start(bf16[3,8,2048]{2,1,0:T(8,128)(2,1)S(1)} %get-tuple-element.28), channel_id=1, source_target_pairs={{0,4},{4,0},{8,12},{12,8},{1,5},{5,1},{9,13},{13,9},{2,6},{6,2},{1... | collective-permute-start | bytes 294920 | tf_op jit(solution)/shard_map/ppermute | solution.py:306
  7.0 1.6 %load.1 = (bf16[2048,256]{1,0:T(8,128)(2,1)S(1)}, bf16[2048,256]{1,0:T(8,128)(2,1)S(1)}) custom-call(bf16[2048,256]{1,0:T(8,128)(2,1)} %bitcast.9, bf16[2048,256]{1,0:T(8,128)(2,1)} %bitcast.10), custom_call_target="tpu_custom_call" | custom-call | flops 500000000 | bytes 2097152 | tf_op jit(solution)/shard_map/load/pallas_call | solution.py:362
  8.5 1.5 %collective-permute-done.4.q_ref = bf16[3,8,2048]{2,1,0:T(8,128)(2,1)S(1)} collective-permute-done((bf16[3,8,2048]{2,1,0:T(8,128)(2,1)S(1)}, bf16[3,8,2048]{2,1,0:T(8,128)(2,1)S(1)}, u32[]{:S(2)}, u32[]{:S(2)}) %collective-permute-start.4) | collective-permute-done | bytes 98336 | tf_op jit(solution)/shard_map/ppermute | solution.py:306
  10.0 1.3 %prompt.7 = bf16[8,6272]{1,0:T(8,128)(2,1)S(1)} custom-call(bf16[3,8,2048]{2,1,0:T(8,128)(2,1)S(1)} %collective-permute-done.4.q_ref, bf16[2048,256]{1,0:T(8,128)(2,1)S(1)} %get-tuple-element.26.k_ref, bf16[2048,256]{1,0:T(8,128)(2,1)S(1)} %get-tuple-element.27.v_ref), custom_call_target="tpu_custom_call" | custom-call | flops 402653184 | bytes 2097152 | tf_op jit(solution)/shard_map/prompt/pallas_call | solution.py:413
  11.4 3.8 %collective-permute-start.5 = (bf16[8,6272]{1,0:T(8,128)(2,1)S(1)}, bf16[8,6272]{1,0:T(8,128)(2,1)S(1)}, u32[]{:S(2)}, u32[]{:S(2)}) collective-permute-start(bf16[8,6272]{1,0:T(8,128)(2,1)S(1)} %prompt.7), channel_id=1, source_target_pairs={{0,12},{4,8},{8,4},{12,0},{1,13},{5,9},{9,5},{13,1},{2,14},{6,10},... | collective-permute-start | bytes 301064 | tf_op jit(solution)/shard_map/ppermute | solution.py:306
  15.2 0.8 %collective-permute-done.2.q_ref = bf16[3,8,2048]{2,1,0:T(8,128)(2,1)S(1)} collective-permute-done((bf16[3,8,2048]{2,1,0:T(8,128)(2,1)S(1)}, bf16[3,8,2048]{2,1,0:T(8,128)(2,1)S(1)}, u32[]{:S(2)}, u32[]{:S(2)}) %collective-permute-start.2) | collective-permute-done | bytes 98336 | tf_op jit(solution)/shard_map/ppermute | solution.py:306
  15.9 1.3 %prompt.6 = bf16[8,6272]{1,0:T(8,128)(2,1)S(1)} custom-call(bf16[3,8,2048]{2,1,0:T(8,128)(2,1)S(1)} %collective-permute-done.2.q_ref, bf16[2048,256]{1,0:T(8,128)(2,1)S(1)} %get-tuple-element.26.k_ref, bf16[2048,256]{1,0:T(8,128)(2,1)S(1)} %get-tuple-element.27.v_ref), custom_call_target="tpu_custom_call" | custom-call | flops 402653184 | bytes 2097152 | tf_op jit(solution)/shard_map/prompt/pallas_call | solution.py:413
  17.3 1.0 %collective-permute-start.3 = (bf16[8,6272]{1,0:T(8,128)(2,1)S(1)}, bf16[8,6272]{1,0:T(8,128)(2,1)S(1)}, u32[]{:S(2)}, u32[]{:S(2)}) collective-permute-start(bf16[8,6272]{1,0:T(8,128)(2,1)S(1)} %prompt.6), channel_id=1, source_target_pairs={{0,8},{4,12},{8,0},{12,4},{1,9},{5,13},{9,1},{13,5},{2,10},{6,14},... | collective-permute-start | bytes 301064 | tf_op jit(solution)/shard_map/ppermute | solution.py:306
  18.2 0.0 collective-permute-done.q_ref
  18.2 0.0 slice-start
  18.2 1.3 %prompt.5 = bf16[8,6272]{1,0:T(8,128)(2,1)S(1)} custom-call(bf16[3,8,2048]{2,1,0:T(8,128)(2,1)S(1)} %collective-permute-done.q_ref, bf16[2048,256]{1,0:T(8,128)(2,1)S(1)} %get-tuple-element.26.k_ref, bf16[2048,256]{1,0:T(8,128)(2,1)S(1)} %get-tuple-element.27.v_ref), custom_call_target="tpu_custom_call" | custom-call | flops 402653184 | bytes 2097152 | tf_op jit(solution)/shard_map/prompt/pallas_call | solution.py:413
  19.6 2.7 %collective-permute-start.1 = (bf16[8,6272]{1,0:T(8,128)(2,1)S(1)}, bf16[8,6272]{1,0:T(8,128)(2,1)S(1)}, u32[]{:S(2)}, u32[]{:S(2)}) collective-permute-start(bf16[8,6272]{1,0:T(8,128)(2,1)S(1)} %prompt.5), channel_id=1, source_target_pairs={{0,4},{4,0},{8,12},{12,8},{1,5},{5,1},{9,13},{13,9},{2,6},{6,2},{1... | collective-permute-start | bytes 301064 | tf_op jit(solution)/shard_map/ppermute | solution.py:306
  22.3 0.0 slice-start.1
  22.3 3.7 %suffix.1 = (f32[3,16,2048]{2,1,0:T(8,128)S(1)}, f32[3,16,2048]{2,1,0:T(8,128)S(1)}) custom-call(bf16[3,16,2048]{2,1,0:T(8,128)(2,1)S(1)} %get-tuple-element.31.q_ref, s32[16]{0:T(128)} %len_hbm.1, bf16[16,256,256]{2,1,0:T(8,128)(2,1)} %k_hbm.1, bf16[16,256,256]{2,1,0:T(8,128)(2,1)} %v_hbm.1, bf16[3,16,256]{2,1,0:T(8,128)(2,1)} %bitcast.13, ...), custom_call_target="tpu_custom_call" | custom-call | flops 3000000000 | bytes 4194304 | tf_op jit(solution)/shard_map/suffix/pallas_call | solution.py:372
  26.0 1.3 %prompt.4.refs_1_ = bf16[8,6272]{1,0:T(8,128)(2,1)S(1)} custom-call(bf16[3,8,2048]{2,1,0:T(8,128)(2,1)S(1)} %get-tuple-element.25.q_ref, bf16[2048,256]{1,0:T(8,128)(2,1)S(1)} %get-tuple-element.26.k_ref, bf16[2048,256]{1,0:T(8,128)(2,1)S(1)} %get-tuple-element.27.v_ref), custom_call_target="tpu_custom_call" | custom-call | flops 402653184 | bytes 2097152 | tf_op jit(solution)/shard_map/prompt/pallas_call | solution.py:413
  27.3 0.0 collective-permute-done.5.refs_4_
  27.3 0.0 collective-permute-done.3.refs_3_
  27.3 0.0 collective-permute-done.1.refs_2_
  27.3 0.5 merge.1.own_ref
  27.8 0.6 %collective-permute-start.7 = (bf16[3,16,2048]{2,1,0:T(8,128)(2,1)S(1)}, bf16[3,16,2048]{2,1,0:T(8,128)(2,1)S(1)}, u32[]{:S(2)}, u32[]{:S(2)}) collective-permute-start(bf16[3,16,2048]{2,1,0:T(8,128)(2,1)S(1)} %merge.1.own_ref), channel_id=1, source_target_pairs={{0,8},{4,12},{8,0},{12,4},{1,9},{5,13},{9,1},{13,5},{2,10},{6,14},... | collective-permute-start | bytes 589832 | tf_op jit(solution)/shard_map/ppermute | solution.py:306
  28.4 0.9 %collective-permute-start.6 = (bf16[3,16,2048]{2,1,0:T(8,128)(2,1)S(1)}, bf16[3,16,2048]{2,1,0:T(8,128)(2,1)S(1)}, u32[]{:S(2)}, u32[]{:S(2)}) collective-permute-start(bf16[3,16,2048]{2,1,0:T(8,128)(2,1)S(1)} %merge.1.own_ref), channel_id=1, source_target_pairs={{0,4},{4,0},{8,12},{12,8},{1,5},{5,1},{9,13},{13,9},{2,6},{6,2},{1... | collective-permute-start | bytes 589832 | tf_op jit(solution)/shard_map/ppermute | solution.py:306
  29.3 6.9 %collective-permute-done.7.g2_ref = bf16[3,16,2048]{2,1,0:T(8,128)(2,1)S(1)} collective-permute-done((bf16[3,16,2048]{2,1,0:T(8,128)(2,1)S(1)}, bf16[3,16,2048]{2,1,0:T(8,128)(2,1)S(1)}, u32[]{:S(2)}, u32[]{:S(2)}) %collective-permute-start.7) | collective-permute-done | bytes 196640 | tf_op jit(solution)/shard_map/ppermute | solution.py:306
  36.1 0.1 collective-permute-done.6.g1_ref
  36.2 0.0 slice-done
  36.2 0.0 slice-done.1
  36.2 1.8 %shard_map.100 = (f32[3,16,2048]{2,1,0:T(8,128)S(1)}, f32[3,16,2048]{2,1,0:T(8,128)S(1)}, bf16[2,3,16,2048]{3,2,1,0:T(8,128)(2,1)S(1)}) custom-call(bf16[3,16,2048]{2,1,0:T(8,128)(2,1)S(1)} %merge.1.own_ref, bf16[3,16,2048]{2,1,0:T(8,128)(2,1)S(1)} %collective-permute-done.6.g1_ref, bf16[3,16,2048]{2,1,0:T(8,128)(2,1)S(1)} %collective-permute-done.7.g2_ref, ...), custom_call_target="tpu_custom_call" | custom-call | flops 1610612736 | bytes 1048576 | tf_op jit(solution)/shard_map/pallas_call | solution.py:448
  38.0 0.1 collective-permute-start.8
  38.1 0.1 collective-permute-start.10
  38.2 7.2 %collective-permute-done.10.rows_ref = bf16[3,16,2048]{2,1,0:T(8,128)(2,1)S(1)} collective-permute-done((bf16[3,16,2048]{2,1,0:T(8,128)(2,1)S(1)}, bf16[3,16,2048]{2,1,0:T(8,128)(2,1)S(1)}, u32[]{:S(2)}, u32[]{:S(2)}) %collective-permute-start.10) | collective-permute-done | bytes 196640 | tf_op jit(solution)/shard_map/ppermute | solution.py:306
  45.4 1.5 %shard_map.102 = (f32[3,16,1024]{2,1,0:T(8,128)S(1)}, bf16[3,16,1024]{2,1,0:T(8,128)(2,1)S(1)}) custom-call(bf16[3,16,2048]{2,1,0:T(8,128)(2,1)S(1)} %collective-permute-done.10.rows_ref, bf16[2048,2048]{1,0:T(8,128)(2,1)S(1)} %bitcast.8), custom_call_target="tpu_custom_call" | custom-call | flops 402653184 | bytes 1048576 | tf_op jit(solution)/shard_map/pallas_call | solution.py:448
  47.0 0.0 collective-permute-start.11
  47.0 1.3 %collective-permute-done.11.got_ref = bf16[3,16,1024]{2,1,0:T(8,128)(2,1)S(1)} collective-permute-done((bf16[3,16,1024]{2,1,0:T(8,128)(2,1)S(1)}, bf16[3,16,1024]{2,1,0:T(8,128)(2,1)S(1)}, u32[]{:S(2)}, u32[]{:S(2)}) %collective-permute-start.11) | collective-permute-done | bytes 98336 | tf_op jit(solution)/shard_map/ppermute | solution.py:306
  48.3 1.6 %collective-permute-start.12 = (bf16[3,16,1024]{2,1,0:T(8,128)(2,1)S(1)}, bf16[3,16,1024]{2,1,0:T(8,128)(2,1)S(1)}, u32[]{:S(2)}, u32[]{:S(2)}) collective-permute-start(bf16[3,16,1024]{2,1,0:T(8,128)(2,1)S(1)} %get-tuple-element.40), channel_id=1, source_target_pairs={{0,2},{1,3},{2,0},{3,1},{4,6},{5,7},{6,4},{7,5},{8,10},{9,11},{10,... | collective-permute-start | bytes 294920 | tf_op jit(solution)/shard_map/ppermute | solution.py:306
  49.9 0.0 collective-permute-done.8.got_ref
  49.9 0.6 %collective-permute-start.9 = (bf16[3,16,2048]{2,1,0:T(8,128)(2,1)S(1)}, bf16[3,16,2048]{2,1,0:T(8,128)(2,1)S(1)}, u32[]{:S(2)}, u32[]{:S(2)}) collective-permute-start(bf16[3,16,2048]{2,1,0:T(8,128)(2,1)S(1)} %shard_map.101), channel_id=1, source_target_pairs={{0,2},{1,3},{2,0},{3,1},{4,6},{5,7},{6,4},{7,5},{8,10},{9,11},{10,... | collective-permute-start | bytes 589832 | tf_op jit(solution)/shard_map/ppermute | solution.py:306
  50.5 3.5 %collective-permute-done.12.got_ref = bf16[3,16,1024]{2,1,0:T(8,128)(2,1)S(1)} collective-permute-done((bf16[3,16,1024]{2,1,0:T(8,128)(2,1)S(1)}, bf16[3,16,1024]{2,1,0:T(8,128)(2,1)S(1)}, u32[]{:S(2)}, u32[]{:S(2)}) %collective-permute-start.12) | collective-permute-done | bytes 98336 | tf_op jit(solution)/shard_map/ppermute | solution.py:306
  54.1 0.1 collective-permute-start.13
  54.1 1.3 %collective-permute-done.13.other_ref = bf16[3,16,1024]{2,1,0:T(8,128)(2,1)S(1)} collective-permute-done((bf16[3,16,1024]{2,1,0:T(8,128)(2,1)S(1)}, bf16[3,16,1024]{2,1,0:T(8,128)(2,1)S(1)}, u32[]{:S(2)}, u32[]{:S(2)}) %collective-permute-start.13) | collective-permute-done | bytes 98336 | tf_op jit(solution)/shard_map/ppermute | solution.py:306
  55.4 2.0 %collective-permute-done.9.came_ref = bf16[3,16,2048]{2,1,0:T(8,128)(2,1)S(1)} collective-permute-done((bf16[3,16,2048]{2,1,0:T(8,128)(2,1)S(1)}, bf16[3,16,2048]{2,1,0:T(8,128)(2,1)S(1)}, u32[]{:S(2)}, u32[]{:S(2)}) %collective-permute-start.9) | collective-permute-done | bytes 196640 | tf_op jit(solution)/shard_map/ppermute | solution.py:306
  57.5 0.8 %shard_map.105 = bf16[3,16,2048]{2,1,0:T(8,128)(2,1)} custom-call(f32[3,16,2048]{2,1,0:T(8,128)S(1)} %get-tuple-element.34.own_ref, bf16[2,3,16,2048]{3,2,1,0:T(8,128)(2,1)S(1)} %collective-permute-done.8.got_ref, bf16[3,16,2048]{2,1,0:T(8,128)(2,1)S(1)} %collective-permute-done.9.came_ref, f32[3,16,1024]{2,1,0:T(8,128)S(1)} %get-tuple-element.41.half_ref, ...), custom_call_target="tpu_custom_call" | custom-call | flops 1048576 | bytes 1048576 | tf_op jit(solution)/shard_map/pallas_call | solution.py:448
  (4 shorter events, 0.1 us)
Async XLA Ops:
  1.2 8.8 %collective-permute-start.4 = (bf16[3,8,2048]{2,1,0:T(8,128)(2,1)S(1)}, bf16[3,8,2048]{2,1,0:T(8,128)(2,1)S(1)}, u32[]{:S(2)}, u32[]{:S(2)}) collective-permute-start(bf16[3,8,2048]{2,1,0:T(8,128)(2,1)S(1)} %get-tuple-element.30), channel_id=1, source_target_pairs={{0,12},{4,8},{8,4},{12,0},{1,13},{5,9},{9,5},{13,1},{2,14},{6,10},... | collective-permute-start | bytes 294920 | tf_op jit(solution)/shard_map/ppermute | solution.py:306
  6.3 9.6 %collective-permute-start.2 = (bf16[3,8,2048]{2,1,0:T(8,128)(2,1)S(1)}, bf16[3,8,2048]{2,1,0:T(8,128)(2,1)S(1)}, u32[]{:S(2)}, u32[]{:S(2)}) collective-permute-start(bf16[3,8,2048]{2,1,0:T(8,128)(2,1)S(1)} %get-tuple-element.29), channel_id=1, source_target_pairs={{0,8},{4,12},{8,0},{12,4},{1,9},{5,13},{9,1},{13,5},{2,10},{6,14},... | collective-permute-start | bytes 294920 | tf_op jit(solution)/shard_map/ppermute | solution.py:306
  6.3 11.9 %collective-permute-start = (bf16[3,8,2048]{2,1,0:T(8,128)(2,1)S(1)}, bf16[3,8,2048]{2,1,0:T(8,128)(2,1)S(1)}, u32[]{:S(2)}, u32[]{:S(2)}) collective-permute-start(bf16[3,8,2048]{2,1,0:T(8,128)(2,1)S(1)} %get-tuple-element.28), channel_id=1, source_target_pairs={{0,4},{4,0},{8,12},{12,8},{1,5},{5,1},{9,13},{13,9},{2,6},{6,2},{1... | collective-permute-start | bytes 294920 | tf_op jit(solution)/shard_map/ppermute | solution.py:306
  11.4 15.9 %collective-permute-start.5 = (bf16[8,6272]{1,0:T(8,128)(2,1)S(1)}, bf16[8,6272]{1,0:T(8,128)(2,1)S(1)}, u32[]{:S(2)}, u32[]{:S(2)}) collective-permute-start(bf16[8,6272]{1,0:T(8,128)(2,1)S(1)} %prompt.7), channel_id=1, source_target_pairs={{0,12},{4,8},{8,4},{12,0},{1,13},{5,9},{9,5},{13,1},{2,14},{6,10},... | collective-permute-start | bytes 301064 | tf_op jit(solution)/shard_map/ppermute | solution.py:306
  17.3 10.0 %collective-permute-start.3 = (bf16[8,6272]{1,0:T(8,128)(2,1)S(1)}, bf16[8,6272]{1,0:T(8,128)(2,1)S(1)}, u32[]{:S(2)}, u32[]{:S(2)}) collective-permute-start(bf16[8,6272]{1,0:T(8,128)(2,1)S(1)} %prompt.6), channel_id=1, source_target_pairs={{0,8},{4,12},{8,0},{12,4},{1,9},{5,13},{9,1},{13,5},{2,10},{6,14},... | collective-permute-start | bytes 301064 | tf_op jit(solution)/shard_map/ppermute | solution.py:306
  18.2 18.0 %slice-start = ((s8[8388608]{0:T(1024)(128)(4,1)}), s8[4194304]{0:T(1024)(128)(4,1)S(1)}, s32[]{:S(2)}) async-start(s8[8388608]{0:T(1024)(128)(4,1)} %bitcast.7), calls=%async_computation | async-start | bytes 8388608
  19.6 7.8 %collective-permute-start.1 = (bf16[8,6272]{1,0:T(8,128)(2,1)S(1)}, bf16[8,6272]{1,0:T(8,128)(2,1)S(1)}, u32[]{:S(2)}, u32[]{:S(2)}) collective-permute-start(bf16[8,6272]{1,0:T(8,128)(2,1)S(1)} %prompt.5), channel_id=1, source_target_pairs={{0,4},{4,0},{8,12},{12,8},{1,5},{5,1},{9,13},{13,9},{2,6},{6,2},{1... | collective-permute-start | bytes 301064 | tf_op jit(solution)/shard_map/ppermute | solution.py:306
  22.3 13.9 %slice-start.1 = ((s8[8388608]{0:T(1024)(128)(4,1)}), s8[4194304]{0:T(1024)(128)(4,1)S(1)}, s32[]{:S(2)}) async-start(s8[8388608]{0:T(1024)(128)(4,1)} %bitcast.7), calls=%async_computation.1 | async-start | bytes 8388608
  27.8 8.3 %collective-permute-start.7 = (bf16[3,16,2048]{2,1,0:T(8,128)(2,1)S(1)}, bf16[3,16,2048]{2,1,0:T(8,128)(2,1)S(1)}, u32[]{:S(2)}, u32[]{:S(2)}) collective-permute-start(bf16[3,16,2048]{2,1,0:T(8,128)(2,1)S(1)} %merge.1.own_ref), channel_id=1, source_target_pairs={{0,8},{4,12},{8,0},{12,4},{1,9},{5,13},{9,1},{13,5},{2,10},{6,14},... | collective-permute-start | bytes 589832 | tf_op jit(solution)/shard_map/ppermute | solution.py:306
  28.4 7.8 %collective-permute-start.6 = (bf16[3,16,2048]{2,1,0:T(8,128)(2,1)S(1)}, bf16[3,16,2048]{2,1,0:T(8,128)(2,1)S(1)}, u32[]{:S(2)}, u32[]{:S(2)}) collective-permute-start(bf16[3,16,2048]{2,1,0:T(8,128)(2,1)S(1)} %merge.1.own_ref), channel_id=1, source_target_pairs={{0,4},{4,0},{8,12},{12,8},{1,5},{5,1},{9,13},{13,9},{2,6},{6,2},{1... | collective-permute-start | bytes 589832 | tf_op jit(solution)/shard_map/ppermute | solution.py:306
  38.0 11.8 %collective-permute-start.8 = (bf16[2,3,16,2048]{3,2,1,0:T(8,128)(2,1)S(1)}, bf16[2,3,16,2048]{3,2,1,0:T(8,128)(2,1)S(1)}, u32[]{:S(2)}, u32[]{:S(2)}) collective-permute-start(bf16[2,3,16,2048]{3,2,1,0:T(8,128)(2,1)S(1)} %get-tuple-element.35), channel_id=1, source_target_pairs={{0,1},{1,0},{2,3},{3,2},{4,5},{5,4},{6,7},{7,6},{8,9},{9,8},{10,11... | collective-permute-start | bytes 1179656 | tf_op jit(solution)/shard_map/ppermute | solution.py:306
  38.1 7.3 %collective-permute-start.10 = (bf16[3,16,2048]{2,1,0:T(8,128)(2,1)S(1)}, bf16[3,16,2048]{2,1,0:T(8,128)(2,1)S(1)}, u32[]{:S(2)}, u32[]{:S(2)}) collective-permute-start(bf16[3,16,2048]{2,1,0:T(8,128)(2,1)S(1)} %collective-permute-done.7.g2_ref), channel_id=1, source_target_pairs={{0,4},{4,0},{8,12},{12,8},{1,5},{5,1},{9,13},{13,9},{2,6},{6,2},{1... | collective-permute-start | bytes 589832 | tf_op jit(solution)/shard_map/ppermute | solution.py:306
  47.0 1.3 %collective-permute-start.11 = (bf16[3,16,1024]{2,1,0:T(8,128)(2,1)S(1)}, bf16[3,16,1024]{2,1,0:T(8,128)(2,1)S(1)}, u32[]{:S(2)}, u32[]{:S(2)}) collective-permute-start(bf16[3,16,1024]{2,1,0:T(8,128)(2,1)S(1)} %get-tuple-element.38), channel_id=1, source_target_pairs={{0,1},{1,0},{2,3},{3,2},{4,5},{5,4},{6,7},{7,6},{8,9},{9,8},{10,11... | collective-permute-start | bytes 294920 | tf_op jit(solution)/shard_map/ppermute | solution.py:306
  48.3 5.7 %collective-permute-start.12 = (bf16[3,16,1024]{2,1,0:T(8,128)(2,1)S(1)}, bf16[3,16,1024]{2,1,0:T(8,128)(2,1)S(1)}, u32[]{:S(2)}, u32[]{:S(2)}) collective-permute-start(bf16[3,16,1024]{2,1,0:T(8,128)(2,1)S(1)} %get-tuple-element.40), channel_id=1, source_target_pairs={{0,2},{1,3},{2,0},{3,1},{4,6},{5,7},{6,4},{7,5},{8,10},{9,11},{10,... | collective-permute-start | bytes 294920 | tf_op jit(solution)/shard_map/ppermute | solution.py:306
  49.9 7.5 %collective-permute-start.9 = (bf16[3,16,2048]{2,1,0:T(8,128)(2,1)S(1)}, bf16[3,16,2048]{2,1,0:T(8,128)(2,1)S(1)}, u32[]{:S(2)}, u32[]{:S(2)}) collective-permute-start(bf16[3,16,2048]{2,1,0:T(8,128)(2,1)S(1)} %shard_map.101), channel_id=1, source_target_pairs={{0,2},{1,3},{2,0},{3,1},{4,6},{5,7},{6,4},{7,5},{8,10},{9,11},{10,... | collective-permute-start | bytes 589832 | tf_op jit(solution)/shard_map/ppermute | solution.py:306
  54.1 1.4 %collective-permute-start.13 = (bf16[3,16,1024]{2,1,0:T(8,128)(2,1)S(1)}, bf16[3,16,1024]{2,1,0:T(8,128)(2,1)S(1)}, u32[]{:S(2)}, u32[]{:S(2)}) collective-permute-start(bf16[3,16,1024]{2,1,0:T(8,128)(2,1)S(1)} %get-tuple-element.42), channel_id=1, source_target_pairs={{0,1},{1,0},{2,3},{3,2},{4,5},{5,4},{6,7},{7,6},{8,9},{9,8},{10,11... | collective-permute-start | bytes 294920 | tf_op jit(solution)/shard_map/ppermute | solution.py:306
